TPU v7x, 32 devices: a whole 2x2x4 slice. The times are simulated.
32 devices in a mesh: seq: 4 (over y, core), head: 8 (over z, x).
Axes of the slice: x: 2, y: 2, z: 4, core: 2. Of those that a mesh axis runs over, the one named last changes fastest.
Arguments:
- queries: bfloat16 [8, 2048, 256], P('head', 'seq'), may hold values from -6 to 6
- keys: bfloat16 [1, 2048, 256], P(None, 'seq'), may hold values from -6 to 6
- values: bfloat16 [1, 2048, 256], P(None, 'seq'), may hold values from -6 to 6
- d_out: bfloat16 [8, 2048, 256], P('head', 'seq'), may hold values from -12 to 12
- doc_lengths: int32 [1, 8], replicated, may hold values from 1 to 768, 2048 in all within a row
- fold_order: int32 [8], replicated, may hold values from 0 to 7, each once
Outputs:
- grad_queries: bfloat16 [8, 2048, 256], P('head', 'seq')
- grad_keys: float32 [1, 2048, 256], P(None, ('seq', 'head'))
- grad_values: float32 [1, 2048, 256], P(None, ('seq', 'head'))
Inputs may be any that keep to these rules, and one draw needn't show every extreme that they name: `doc_lengths`: each row's 8 lengths are at least 1, sum to 2048, and the longest is exactly 768. fold_order names each of 0 to 7 once.
All inputs are finite; a program needn't handle non-finite values.
Results may differ from a plain program's by a relative error of at most 0.029.
Values may be sent and summed in bfloat16 or wider, within the bound.
No kernel may reach another device: no remote copies, remote signals or barrier semaphores. Data moves between devices by JAX's collectives and lax.ppermute only.
A program may use at most 64 MiB of HBM per device.

v0:
```python
import jax
import jax.numpy as jnp
from jax import lax
from jax.sharding import PartitionSpec as P

HEAD_COUNT = 8


masked_value = -1e30


def contract_last(left, right):
    return lax.dot_general(
        left, right, (((1,), (1,)), ((), ())), preferred_element_type=jnp.float32
    )


def contract_first(left, right):
    return lax.dot_general(
        left, right, (((0,), (0,)), ((), ())), preferred_element_type=jnp.float32
    )


def block_grads(query_rows, grad_out, log_norm, grad_dot, key_part, value_part, allowed, scaling):
    scores = contract_last(query_rows, key_part) * scaling
    weights = jnp.exp(jnp.where(allowed, scores - log_norm, masked_value))
    weights_low = weights.astype(jnp.bfloat16)
    grad_prob = contract_last(grad_out, value_part)
    grad_score = (weights * (grad_prob - grad_dot)).astype(jnp.bfloat16)
    part_query = jnp.dot(grad_score, key_part, preferred_element_type=jnp.float32) * scaling
    part_key = contract_first(grad_score, query_rows) * scaling
    part_value = contract_first(weights_low, grad_out)
    return (part_query, part_key, part_value)


def owner_blocks(key_part, value_part, row_count):
    head_total = lax.axis_size("head")
    piece_len = key_part.shape[0] // head_total
    width = key_part.shape[1]
    moved = (
        lax.all_to_all(
            key_part.astype(jnp.bfloat16), "head", split_axis=0, concat_axis=0, tiled=True
        ).astype(key_part.dtype),
        lax.all_to_all(
            value_part.astype(jnp.bfloat16), "head", split_axis=0, concat_axis=0, tiled=True
        ).astype(value_part.dtype),
    )
    return tuple(
        (
            jnp.sum(item.reshape(row_count, head_total // row_count, piece_len, width), axis=1)
            for item in moved
        )
    )


def per_device(queries, keys, values, d_out, doc_lengths, fold_order):
    local_len = queries.shape[1]
    head_width = queries.shape[2]
    half_len = local_len // 2
    scaling = head_width ** (-0.5)
    seq_index = lax.axis_index("seq")
    row_index = lax.axis_index("head") // HEAD_COUNT
    row_count = keys.shape[0]
    span_ids = jnp.arange(fold_order.shape[0], dtype=jnp.int32)
    lengths = lax.dynamic_index_in_dim(doc_lengths, row_index, 0, keepdims=False)
    starts = jnp.cumsum(lengths, dtype=jnp.int32) - lengths

    def locate(indices):
        block_of = indices // half_len
        anchor = jnp.sum(
            jnp.where(block_of[:, None] == span_ids[None, :], fold_order[None, :], 0),
            axis=1,
            dtype=jnp.int32,
        )
        position = anchor * half_len + indices % half_len
        document = jnp.sum(
            (position[:, None] >= starts[None, :]).astype(jnp.int32), axis=1, dtype=jnp.int32
        )
        return (position, document)

    def allowed_pairs(query_place, key_place):
        return (query_place[1][:, None] == key_place[1][None, :]) & (
            key_place[0][None, :] <= query_place[0][:, None]
        )

    local_rows = jnp.arange(local_len, dtype=jnp.int32)
    own_place = locate(seq_index * local_len + local_rows)
    query_rows = queries[0]
    grad_out = d_out[0]
    key_row = lax.dynamic_index_in_dim(keys, row_index, 0, keepdims=False)
    value_row = lax.dynamic_index_in_dim(values, row_index, 0, keepdims=False)
    key_part = lax.all_gather(key_row, "seq", axis=0, tiled=True)
    value_part = lax.all_gather(value_row, "seq", axis=0, tiled=True)
    allowed = allowed_pairs(own_place, locate(jnp.arange(key_part.shape[0], dtype=jnp.int32)))
    run_max = jnp.full((local_len, 1), masked_value, jnp.float32)
    scores = jnp.where(allowed, contract_last(query_rows, key_part) * scaling, masked_value)
    new_max = jnp.maximum(run_max, jnp.max(scores, axis=1, keepdims=True))
    weights = jnp.where(allowed, jnp.exp(scores - new_max), 0.0)
    sum_next = jnp.sum(weights, axis=1, keepdims=True)
    acc_next = jnp.dot(weights.astype(jnp.bfloat16), value_part, preferred_element_type=jnp.float32)
    log_norm = new_max + jnp.log(sum_next)
    output = acc_next / sum_next
    grad_dot = jnp.sum(grad_out.astype(jnp.float32) * output, axis=1, keepdims=True)
    key_part = lax.all_gather(key_row, "seq", axis=0, tiled=True)
    value_part = lax.all_gather(value_row, "seq", axis=0, tiled=True)
    row_total = key_part.shape[0]
    allowed = allowed_pairs(own_place, locate(jnp.arange(row_total, dtype=jnp.int32)))
    part_query, part_key, part_value = block_grads(
        query_rows, grad_out, log_norm, grad_dot, key_part, value_part, allowed, scaling
    )
    full_keys = part_key
    full_values = part_value
    grad_query, full_keys, full_values = (part_query, full_keys, full_values)
    seq_keys, seq_values = (
        lax.psum_scatter(
            full_keys.astype(jnp.bfloat16), "seq", scatter_dimension=0, tiled=True
        ).astype(jnp.float32),
        lax.psum_scatter(
            full_values.astype(jnp.bfloat16), "seq", scatter_dimension=0, tiled=True
        ).astype(jnp.float32),
    )
    grad_keys, grad_values = owner_blocks(seq_keys, seq_values, row_count)
    grad_queries = grad_query.astype(jnp.bfloat16)[None]
    return (grad_queries, grad_keys, grad_values)


def solution(mesh):
    in_specs = (
        P("head", "seq", None),
        P(None, "seq", None),
        P(None, "seq", None),
        P("head", "seq", None),
        P(),
        P(),
    )
    out_specs = (
        P("head", "seq", None),
        P(None, ("seq", "head"), None),
        P(None, ("seq", "head"), None),
    )
    return jax.shard_map(
        per_device, mesh=mesh, in_specs=in_specs, out_specs=out_specs, check_vma=False
    )
```

profile of v0, /device:TPU:0, one launch (start us, length us, event | category | flops | bytes accessed | tf_op | source)
XLA Modules:
  0.0 123.3 jit_solution(2231959383606064671)
XLA Ops:
  7.2 0.0 copy-start
  7.2 0.0 all-gather.5.cloned.1.call-start
  7.2 0.7 all-gather.5.cloned.1.call-update
  7.9 0.0 all-gather.7.cloned.1.call-start
  8.0 0.7 all-gather.7.cloned.1.call-update
  8.7 0.0 reduce-scatter.5.cloned.1.call-start
  8.7 0.8 reduce-window_clone.1
  9.6 0.7 subtract_bitcast_fusion
  10.2 0.7 select_reduce_fusion.1
  11.0 0.7 select_reduce_fusion
  11.7 0.1 convert_reduce_fusion.3
  11.8 0.1 convert_reduce_fusion.2
  11.9 17.1 %all-gather.5.cloned.1.call-done = bf16[1,2048,256]{2,1,0:T(8,128)(2,1)} async-done(((bf16[1,512,256]{2,1,0:T(8,128)(2,1)}), bf16[1,2048,256]{2,1,0:T(8,128)(2,1)}) %all-gather.5.cloned.1.call-update) | async-done | bytes 1048592 | tf_op jit(solution)/shard_map/all_gather | solution.py:104
  29.0 0.0 copy-done
  29.0 2.6 %fusion = (f32[512]{0:T(512)S(1)}, f32[512,2048]{1,0:T(8,128)S(1)}) fusion(s32[512]{0:T(512)S(1)} %fusion.45, s32[2048]{0:T(1024)S(1)} %fusion.43, s32[2048]{0:T(1024)S(1)} %convert_reduce_fusion.2, s32[512]{0:T(512)S(1)} %convert_reduce_fusion.3, bf16[1,2048,256]{2,1,0:T(8,128)(2,1)} %all-gather.5.cloned.1.call-done, bf16[1,512,256]{2,1,0:T(8,128)(2,1)S(1)} %copy-done), kind=kOutput, calls=%fused_computation.5 | convolution fusion | flops 543161856 | bytes 5527552 | tf_op jit(solution)/shard_map/dot_general | solution.py:13
  31.6 0.0 copy-start.1
  31.6 0.0 copy-start.3
  31.6 1.7 %fusion.4 = f32[512]{0:T(512)S(1)} fusion(f32[512,2048]{1,0:T(8,128)S(1)} %get-tuple-element.4, f32[512]{0:T(512)S(1)} %broadcast_maximum_fusion, s32[512]{0:T(512)S(1)} %fusion.45, s32[2048]{0:T(1024)S(1)} %fusion.43, s32[2048]{0:T(1024)S(1)} %convert_reduce_fusion.2, s32[512]{0:T(512)S(1)} %convert_reduce_fusion.3), kind=kLoop, calls=%fused_computation.11 | loop fusion | flops 8388096 | bytes 4218880 | tf_op jit(solution)/shard_map/reduce_sum | solution.py:99
  33.3 0.2 copy-done.1
  33.5 0.0 copy-done.3
  33.5 2.9 %convolution_convert_fusion = bf16[2048,256]{1,0:T(8,128)(2,1)} fusion(f32[512,2048]{1,0:T(8,128)S(1)} %get-tuple-element.4, f32[512]{0:T(512)S(1)} %log_add_fusion, bf16[1,512,256]{2,1,0:T(8,128)(2,1)S(1)} %copy-done.3, s32[2048]{0:T(1024)S(1)} %fusion.43, s32[2048]{0:T(1024)S(1)} %convert_reduce_fusion.2, s32[512]{0:T(512)S(1)} %fusion.45, ...), kind=kOutput, calls=%fused_computation.9 | convolution fusion | flops 544735232 | bytes 5527552 | tf_op jit(solution)/shard_map/dot_general | solution.py:19
  36.4 0.0 reduce-scatter.5.cloned.1.call-update
  36.5 0.0 reduce-scatter.3.cloned.1.call-start
  36.5 0.1 copy.10
  36.7 10.6 %all-gather.7.cloned.1.call-done = bf16[1,2048,256]{2,1,0:T(8,128)(2,1)} async-done(((bf16[1,512,256]{2,1,0:T(8,128)(2,1)}), bf16[1,2048,256]{2,1,0:T(8,128)(2,1)}) %all-gather.7.cloned.1.call-update) | async-done | bytes 1048592 | tf_op jit(solution)/shard_map/all_gather | solution.py:105
  47.3 0.0 copy-start.2
  47.3 0.0 copy-start.5
  47.3 4.2 %fusion.28 = f32[512]{0:T(512)S(1)} fusion(bf16[1,2048,256]{2,1,0:T(8,128)(2,1)} %all-gather.7.cloned.1.call-done, f32[512,2048]{1,0:T(8,128)} %copy-done.1, f32[512]{0:T(512)S(1)} %broadcast_maximum_fusion, bf16[1,512,256]{1,2,0:T(8,128)(2,1)S(1)} %copy.10, f32[512]{0:T(512)S(1)} %fusion.4, s32[2048]{0:T(1024)S(1)} %fusion.43, ...), kind=kOutput, calls=%fused_computation.26 | convolution fusion | flops 545783296 | bytes 5531648 | tf_op jit(solution)/shard_map/dot_general | solution.py:100
  51.5 0.0 copy-done.2
  51.5 0.0 copy-done.5
  51.5 2.1 %multiply_convert_fusion = bf16[512,2048]{1,0:T(8,128)(2,1)S(1)} fusion(f32[512,2048]{1,0:T(8,128)S(1)} %copy-done.2, f32[512]{0:T(512)S(1)} %fusion.28, f32[512]{0:T(512)S(1)} %log_add_fusion, bf16[1,2048,256]{2,1,0:T(8,128)(2,1)S(1)} %copy-done.5, bf16[1,512,256]{2,1,0:T(8,128)(2,1)S(1)} %copy-done.3, s32[512]{0:T(512)S(1)} %fusion.45, ...), kind=kOutput, calls=%fused_computation | convolution fusion | flops 546308096 | bytes 7626752 | tf_op jit(solution)/shard_map/dot_general | solution.py:13
  53.6 0.0 copy-start.6
  53.6 1.3 %copy-done.6 = bf16[512,2048]{1,0:T(8,128)(2,1)} copy-done((bf16[512,2048]{1,0:T(8,128)(2,1)}, bf16[512,2048]{1,0:T(8,128)(2,1)S(1)}, u32[]{:S(2)}) %copy-start.6) | copy-done | bytes 2097176
  54.9 0.0 copy-start.4
  54.9 1.8 %fusion.2 = bf16[2048,256]{1,0:T(8,128)(2,1)} fusion(bf16[512,2048]{1,0:T(8,128)(2,1)S(1)} %multiply_convert_fusion, bf16[1,512,256]{2,1,0:T(8,128)(2,1)S(1)} %copy-done), kind=kOutput, calls=%fused_computation.8 | convolution fusion | flops 537919488 | bytes 3407872 | tf_op jit(solution)/shard_map/dot_general | solution.py:19
  56.7 0.0 reduce-scatter.3.cloned.1.call-update
  56.7 17.9 %reduce-scatter.5.cloned.1.call-done = bf16[512,256]{1,0:T(8,128)(2,1)} async-done(((bf16[2048,256]{1,0:T(8,128)(2,1)}), bf16[512,256]{1,0:T(8,128)(2,1)}) %reduce-scatter.5.cloned.1.call-update) | async-done | bytes 262160 | tf_op jit(solution)/shard_map/reduce_scatter | solution.py:118
  74.7 5.5 %all-to-all-start.1 = ((bf16[8,64,256]{2,1,0:T(8,128)(2,1)}), bf16[8,64,256]{2,1,0:T(8,128)(2,1)S(1)}, u32[]{:S(2)}, u32[]{:S(2)}) async-start(bf16[8,64,256]{2,1,0:T(8,128)(2,1)} %bitcast.43), calls=%async_computation.3 | async-start | bytes 524288 | tf_op jit(solution)/shard_map/all_to_all | solution.py:44
  80.2 21.7 %reduce-scatter.3.cloned.1.call-done = bf16[512,256]{1,0:T(8,128)(2,1)} async-done(((bf16[2048,256]{1,0:T(8,128)(2,1)}), bf16[512,256]{1,0:T(8,128)(2,1)}) %reduce-scatter.3.cloned.1.call-update) | async-done | bytes 262160 | tf_op jit(solution)/shard_map/reduce_scatter | solution.py:115
  101.9 0.0 all-to-all-done.1
  101.9 5.5 %all-to-all-start = ((bf16[8,64,256]{2,1,0:T(8,128)(2,1)}), bf16[8,64,256]{2,1,0:T(8,128)(2,1)S(1)}, u32[]{:S(2)}, u32[]{:S(2)}) async-start(bf16[8,64,256]{2,1,0:T(8,128)(2,1)} %bitcast.44), calls=%async_computation.1 | async-start | bytes 524288 | tf_op jit(solution)/shard_map/all_to_all | solution.py:41
  107.4 0.0 copy-done.4
  107.4 3.0 %fusion.12 = bf16[1,512,256]{2,1,0:T(8,128)(2,1)} fusion(bf16[512,2048]{1,0:T(8,128)(2,1)} %copy-done.6, bf16[1,2048,256]{2,1,0:T(8,128)(2,1)S(1)} %copy-done.4), kind=kOutput, calls=%fused_computation.18 | convolution fusion | flops 537133056 | bytes 3407872 | tf_op jit(solution)/shard_map/dot_general | solution.py:30
  110.4 0.7 convert_reduce_fusion
  111.1 5.1 %all-to-all-done = bf16[8,64,256]{2,1,0:T(8,128)(2,1)S(1)} async-done(((bf16[8,64,256]{2,1,0:T(8,128)(2,1)}), bf16[8,64,256]{2,1,0:T(8,128)(2,1)S(1)}, u32[]{:S(2)}, u32[]{:S(2)}) %all-to-all-start) | async-done | bytes 262176 | tf_op jit(solution)/shard_map/all_to_all | solution.py:41
  116.1 0.7 convert_reduce_fusion.1
  (6 shorter events, 0.0 us)
Async XLA Ops:
  7.2 21.8 %copy-start = (bf16[1,512,256]{2,1,0:T(8,128)(2,1)S(1)}, bf16[1,512,256]{2,1,0:T(8,128)(2,1)}, u32[]{:S(2)}) copy-start(bf16[1,512,256]{2,1,0:T(8,128)(2,1)} %param.6) | copy-start | bytes 786436
  7.2 21.8 %all-gather.5.cloned.1.call-start = ((), (), s32[]{:S(2)}) async-start(), calls=%async_computation.6 | async-start | bytes 1310720 | tf_op jit(solution)/shard_map/all_gather | solution.py:104
  7.9 39.4 %all-gather.7.cloned.1.call-start = ((), (), s32[]{:S(2)}) async-start(), calls=%async_computation.7 | async-start | bytes 1310720 | tf_op jit(solution)/shard_map/all_gather | solution.py:105
  8.7 66.0 %reduce-scatter.5.cloned.1.call-start = ((), (), s32[]{:S(2)}) async-start(), calls=%async_computation.5 | async-start | bytes 1310720 | tf_op jit(solution)/shard_map/reduce_scatter | solution.py:118
  31.6 1.9 %copy-start.1 = (f32[512,2048]{1,0:T(8,128)}, f32[512,2048]{1,0:T(8,128)S(1)}, u32[]{:S(2)}) copy-start(f32[512,2048]{1,0:T(8,128)S(1)} %get-tuple-element.4) | copy-start | bytes 12582916
  31.6 1.9 %copy-start.3 = (bf16[1,512,256]{2,1,0:T(8,128)(2,1)S(1)}, bf16[1,512,256]{2,1,0:T(8,128)(2,1)}, u32[]{:S(2)}) copy-start(bf16[1,512,256]{2,1,0:T(8,128)(2,1)} %param.9) | copy-start | bytes 786436
  36.5 65.4 %reduce-scatter.3.cloned.1.call-start = ((), (), s32[]{:S(2)}) async-start(), calls=%async_computation.4 | async-start | bytes 1310720 | tf_op jit(solution)/shard_map/reduce_scatter | solution.py:115
  47.3 4.2 %copy-start.2 = (f32[512,2048]{1,0:T(8,128)S(1)}, f32[512,2048]{1,0:T(8,128)}, u32[]{:S(2)}) copy-start(f32[512,2048]{1,0:T(8,128)} %copy-done.1) | copy-start | bytes 12582916
  47.3 4.2 %copy-start.5 = (bf16[1,2048,256]{2,1,0:T(8,128)(2,1)S(1)}, bf16[1,2048,256]{2,1,0:T(8,128)(2,1)}, u32[]{:S(2)}) copy-start(bf16[1,2048,256]{2,1,0:T(8,128)(2,1)} %all-gather.7.cloned.1.call-done) | copy-start | bytes 3145732
  53.6 1.4 %copy-start.6 = (bf16[512,2048]{1,0:T(8,128)(2,1)}, bf16[512,2048]{1,0:T(8,128)(2,1)S(1)}, u32[]{:S(2)}) copy-start(bf16[512,2048]{1,0:T(8,128)(2,1)S(1)} %multiply_convert_fusion) | copy-start | bytes 6291460
  54.9 52.4 %copy-start.4 = (bf16[1,2048,256]{2,1,0:T(8,128)(2,1)S(1)}, bf16[1,2048,256]{2,1,0:T(8,128)(2,1)}, u32[]{:S(2)}) copy-start(bf16[1,2048,256]{2,1,0:T(8,128)(2,1)} %all-gather.5.cloned.1.call-done) | copy-start | bytes 3145732
  74.7 27.2 %all-to-all-start.1 = ((bf16[8,64,256]{2,1,0:T(8,128)(2,1)}), bf16[8,64,256]{2,1,0:T(8,128)(2,1)S(1)}, u32[]{:S(2)}, u32[]{:S(2)}) async-start(bf16[8,64,256]{2,1,0:T(8,128)(2,1)} %bitcast.43), calls=%async_computation.3 | async-start | bytes 524288 | tf_op jit(solution)/shard_map/all_to_all | solution.py:44
  101.9 14.3 %all-to-all-start = ((bf16[8,64,256]{2,1,0:T(8,128)(2,1)}), bf16[8,64,256]{2,1,0:T(8,128)(2,1)S(1)}, u32[]{:S(2)}, u32[]{:S(2)}) async-start(bf16[8,64,256]{2,1,0:T(8,128)(2,1)} %bitcast.44), calls=%async_computation.1 | async-start | bytes 524288 | tf_op jit(solution)/shard_map/all_to_all | solution.py:41
Sparse Core Ops, SparseCore 0:
  9.5 19.4 all-gather.4
  30.6 16.6 all-gather.6
  49.8 24.7 reduce-scatter.4
  77.0 24.7 reduce-scatter.2
where the time goes:
time: 124 us; the launch traced here: 123 us
  waiting for transfers between devices  73.8 us (60%)
  matrix products  16.5 us (13%)
  between operations  13.9 us (11%)
  starting transfers between devices  11.2 us (9%)
  other arithmetic  6.24 us (5%)
  local copies, waits for them, and re-layouts  1.69 us (1%)
    reduce_scatter x1, waiting for transfers between devices, per_device(): lax.psum_scatter(full_keys.astype(jnp.bfloat16), 'seq', scatter_dimension...  21.7 us
    reduce_scatter x1, waiting for transfers between devices, per_device(): lax.psum_scatter(full_values.astype(jnp.bfloat16), 'seq', scatter_dimensi...  17.9 us
    all_gather x1, waiting for transfers between devices, per_device(): key_part = lax.all_gather(key_row, 'seq', axis=0, tiled=True)  17.1 us
    all_gather x1, waiting for transfers between devices, per_device(): value_part = lax.all_gather(value_row, 'seq', axis=0, tiled=True)  10.6 us
    all_to_all x1, starting transfers between devices, owner_blocks(): lax.all_to_all(key_part.astype(jnp.bfloat16), 'head', split_axis=0, conca...  5.51 us
    all_to_all x1, starting transfers between devices, owner_blocks(): lax.all_to_all(value_part.astype(jnp.bfloat16), 'head', split_axis=0, con...  5.51 us
    all_to_all x1, waiting for transfers between devices, owner_blocks(): lax.all_to_all(key_part.astype(jnp.bfloat16), 'head', split_axis=0, conca...  5.07 us
    dot_general x2, matrix products, contract_first(): lax.dot_general(left, right, (((0,), (0,)), ((), ())), preferred_element_...  4.69 us
  transfers between devices with their start and end apart: 6, of which 5 were waited for; matrix products, arithmetic and copies ran while one was open for 18% of the time, Pallas kernels for 0%

commit v1 on v0

v1 whole, which is shorter than its diff:
```python
import functools
import math

import jax
import jax.numpy as jnp
from jax import lax
from jax.experimental import pallas as pl
from jax.experimental.pallas import tpu as pltpu
from jax.sharding import PartitionSpec as P

HEAD_COUNT = 8
MASKED = -1e30
CORES = 2


def contract(left, right, left_dim, right_dim):
    return lax.dot_general(
        left, right, (((left_dim,), (right_dim,)), ((), ())), preferred_element_type=jnp.float32
    )


class Places:
    def __init__(self, docs_ref, fold_ref, local_len):
        seq_total = lax.axis_size("seq")
        self.fold_ref = fold_ref
        self.per_shard = fold_ref.shape[0] // seq_total
        self.block = local_len // self.per_shard
        row = lax.axis_index("head") // HEAD_COUNT
        starts = [jnp.int32(0)]
        for d in range(docs_ref.shape[1] - 1):
            starts.append(starts[-1] + docs_ref[row, d])
        self.starts = starts

    def base(self, shard, index):
        return self.fold_ref[shard * self.per_shard + index] * self.block

    def row_place(self, base):
        position = base + lax.broadcasted_iota(jnp.int32, (1, self.block), 1)
        start = jnp.zeros((1, self.block), jnp.int32)
        first = jnp.int32(0)
        for d in self.starts[1:]:
            start = jnp.where(position >= d, d, start)
            first = jnp.where(base >= d, d, first)
        return position, start, first

    def active(self, query_base, first, key_base):
        return (key_base <= query_base) & (key_base + self.block > first)

    def allowed(self, query_place, key_base):
        position, start, _ = query_place
        key_position = key_base + lax.broadcasted_iota(jnp.int32, (self.block, self.block), 0)
        return (key_position >= start) & (key_position <= position)


def masked_scores(keys, query, allowed, factor):
    return jnp.where(allowed, contract(keys, query, 1, 1) * factor, MASKED)


def shard_at(offset):
    total = lax.axis_size("seq")
    return lax.rem(lax.axis_index("seq") + offset * CORES, total)


def stats_body(offset, factor, docs, fold, query, grad, key_own, value_own, key_sib, value_sib, out):
    place = Places(docs, fold, query.shape[0])
    block = place.block
    own = lax.axis_index("seq")
    query_shard = shard_at(offset)
    for i in range(place.per_shard):
        rows = pl.ds(i * block, block)
        base = place.base(query_shard, i)
        query_place = place.row_place(base)
        out[0:1, rows] = jnp.full((1, block), MASKED, jnp.float32)
        out[1:3, rows] = jnp.zeros((2, block), jnp.float32)
        for shard, keys, values in ((own, key_own, value_own), (own ^ 1, key_sib, value_sib)):
            for j in range(place.per_shard):
                key_base = place.base(shard, j)
                cols = pl.ds(j * block, block)

                @pl.when(place.active(base, query_place[2], key_base))
                def _():
                    scores = masked_scores(
                        keys[cols, :], query[rows, :], place.allowed(query_place, key_base), factor
                    )
                    prob = contract(values[cols, :], grad[rows, :], 1, 1)
                    old_max = out[0:1, rows]
                    new_max = jnp.maximum(old_max, jnp.max(scores, axis=0, keepdims=True))
                    keep = jnp.exp2(old_max - new_max)
                    weights = jnp.exp2(scores - new_max)
                    out[0:1, rows] = new_max
                    out[1:2, rows] = out[1:2, rows] * keep + jnp.sum(weights, axis=0, keepdims=True)
                    out[2:3, rows] = out[2:3, rows] * keep + jnp.sum(
                        weights * prob, axis=0, keepdims=True
                    )


def grads_body(offset, factor, parts, first, last, *refs):
    docs, fold, query, grad, key_own, value_own, key_sib, value_sib = refs[:8]
    stats = refs[8 : 8 + parts]
    rest = list(refs[8 + parts :])
    prior = None if first else (rest.pop(0), rest.pop(0))
    dq = rest.pop(0)
    outs = [rest.pop(0) for _ in range(4 if last else 2)]
    acc_key, acc_value, acc_query = rest
    place = Places(docs, fold, query.shape[0])
    block = place.block
    own = lax.axis_index("seq")
    query_shard = shard_at(offset)
    local = query.shape[0]
    if first:
        acc_key[...] = jnp.zeros_like(acc_key)
        acc_value[...] = jnp.zeros_like(acc_value)
    else:
        acc_key[...] = prior[0][...]
        acc_value[...] = prior[1][...]
    acc_query[...] = jnp.zeros_like(acc_query)
    top = stats[0][0:1, :]
    for part in stats[1:]:
        top = jnp.maximum(top, part[0:1, :])
    total = jnp.zeros_like(top)
    dots = jnp.zeros_like(top)
    for part in stats:
        keep = jnp.exp2(part[0:1, :] - top)
        total = total + part[1:2, :] * keep
        dots = dots + part[2:3, :] * keep
    norm = top + jnp.log2(total)
    dots = dots / total
    for i in range(place.per_shard):
        rows = pl.ds(i * block, block)
        base = place.base(query_shard, i)
        query_place = place.row_place(base)
        norm_i = norm[:, i * block : (i + 1) * block]
        dots_i = dots[:, i * block : (i + 1) * block]
        for side, (shard, keys, values) in enumerate(
            ((own, key_own, value_own), (own ^ 1, key_sib, value_sib))
        ):
            for j in range(place.per_shard):
                key_base = place.base(shard, j)
                cols = pl.ds(j * block, block)
                accs = pl.ds(side * local + j * block, block)

                @pl.when(place.active(base, query_place[2], key_base))
                def _():
                    q, g, k = query[rows, :], grad[rows, :], keys[cols, :]
                    scores = masked_scores(k, q, place.allowed(query_place, key_base), factor)
                    weights = jnp.exp2(scores - norm_i)
                    prob = contract(values[cols, :], g, 1, 1)
                    slope = (weights * (prob - dots_i)).astype(jnp.bfloat16)
                    acc_value[accs, :] += contract(weights.astype(jnp.bfloat16), g, 1, 0)
                    acc_key[accs, :] += contract(slope, q, 1, 0)
                    acc_query[rows, :] += contract(slope, k, 0, 0)

    dq[...] = acc_query[...].astype(dq.dtype)
    if last:
        for acc, mine, other in ((acc_key, outs[0], outs[2]), (acc_value, outs[1], outs[3])):
            mine[...] = acc[0:local, :]
            other[...] = acc[local : 2 * local, :].astype(other.dtype)
    else:
        outs[0][...] = acc_key[...]
        outs[1][...] = acc_value[...]


def pieces_body(scaling, dk, dv, dk_in, dv_in, mine, *outs):
    heads = lax.axis_size("head")
    head = lax.axis_index("head")
    piece = mine.shape[1]
    for step in range(heads):
        target = lax.rem(head + step, heads)
        rows = pl.ds(pl.multiple_of(target * piece, piece), piece)
        key_sum = (dk[rows, :] + dk_in[rows, :].astype(jnp.float32)) * scaling
        value_sum = dv[rows, :] + dv_in[rows, :].astype(jnp.float32)
        out = mine if step == 0 else outs[step - 1]
        out[0] = key_sum.astype(out.dtype)
        out[1] = value_sum.astype(out.dtype)


SMEM = pl.BlockSpec(memory_space=pltpu.SMEM)
VMEM = pl.BlockSpec(memory_space=pltpu.VMEM)


def shift(x, axis, amount):
    size = lax.axis_size(axis)
    return lax.ppermute(x, axis, [(i, (i - amount) % size) for i in range(size)])


def swap_cores(x):
    return lax.ppermute(x, "seq", [(i, i ^ 1) for i in range(lax.axis_size("seq"))])


def per_device(queries, keys, values, d_out, doc_lengths, fold_order):
    local, width = queries.shape[1:]
    chips = lax.axis_size("seq") // CORES
    heads = lax.axis_size("head")
    row_count = keys.shape[0]
    piece = local // heads
    scaling = width ** (-0.5)
    factor = scaling * math.log2(math.e)
    row_index = lax.axis_index("head") // HEAD_COUNT
    if row_count == 1:
        key_own, value_own = keys[0], values[0]
    else:
        key_own = lax.dynamic_index_in_dim(keys, row_index, 0, keepdims=False)
        value_own = lax.dynamic_index_in_dim(values, row_index, 0, keepdims=False)
    sets = [(queries[0], d_out[0])]
    for offset in range(1, chips):
        sets.append(
            (shift(queries[0], "seq", offset * CORES), shift(d_out[0], "seq", offset * CORES))
        )
    key_sib, value_sib = swap_cores(key_own), swap_cores(value_own)
    chip_keys = (key_own, value_own, key_sib, value_sib)
    tiles = local * 2 * local * width

    stats = []
    for offset in range(chips):
        stats.append(
            pl.pallas_call(
                functools.partial(stats_body, offset, factor),
                out_shape=jax.ShapeDtypeStruct((3, local), jnp.float32),
                in_specs=[SMEM] * 2 + [VMEM] * 6,
                out_specs=VMEM,
                name=f"stats{offset}",
                cost_estimate=pl.CostEstimate(
                    flops=4 * tiles, bytes_accessed=6 * local * width * 2, transcendentals=0
                ),
            )(doc_lengths, fold_order, *sets[offset], *chip_keys)
        )
    far = {
        (step, offset): shift(stats[(offset - step) % chips], "seq", step * CORES)
        for step in range(1, chips)
        for offset in range(chips)
    }
    acc = None
    partial_queries = [None] * chips
    order = list(range(1, chips)) + [0]
    for n, offset in enumerate(order):
        first, last = n == 0, n == chips - 1
        parts = [stats[offset]] + [far[step, offset] for step in range(1, chips)]
        wide = jax.ShapeDtypeStruct((CORES * local, width), jnp.float32)
        mine = jax.ShapeDtypeStruct((local, width), jnp.float32)
        sent = jax.ShapeDtypeStruct((local, width), jnp.bfloat16)
        out_shape = [mine if offset == 0 else sent]
        out_shape += [mine, mine, sent, sent] if last else [wide, wide]
        operands = [doc_lengths, fold_order, *sets[offset], *chip_keys, *parts]
        operands += [] if first else list(acc)
        results = pl.pallas_call(
            functools.partial(grads_body, offset, factor, chips, first, last),
            out_shape=out_shape,
            in_specs=[SMEM] * 2 + [VMEM] * (len(operands) - 2),
            out_specs=[VMEM] * len(out_shape),
            scratch_shapes=[
                pltpu.VMEM((CORES * local, width), jnp.float32),
                pltpu.VMEM((CORES * local, width), jnp.float32),
                pltpu.VMEM((local, width), jnp.float32),
            ],
            name=f"grads{offset}",
            cost_estimate=pl.CostEstimate(
                flops=10 * tiles, bytes_accessed=8 * local * width * 4, transcendentals=0
            ),
        )(*operands)
        partial_queries[offset] = results[0]
        acc = results[1:]
    dk, dv, dk_out, dv_out = acc
    dk_in, dv_in = swap_cores(dk_out), swap_cores(dv_out)
    grad_query = partial_queries[0]
    for offset in range(1, chips):
        grad_query = grad_query + shift(
            partial_queries[offset], "seq", -offset * CORES
        ).astype(jnp.float32)
    grad_queries = (grad_query * scaling).astype(jnp.bfloat16)[None]

    moved = pl.pallas_call(
        functools.partial(pieces_body, scaling),
        out_shape=[jax.ShapeDtypeStruct((2, piece, width), jnp.float32)]
        + [jax.ShapeDtypeStruct((2, piece, width), jnp.bfloat16)] * (heads - 1),
        in_specs=[VMEM] * 4,
        out_specs=[VMEM] * heads,
        name="pieces",
        cost_estimate=pl.CostEstimate(
            flops=4 * local * width, bytes_accessed=8 * local * width * 4, transcendentals=0
        ),
    )(dk, dv, dk_in, dv_in)
    terms = [moved[0]]
    for step in range(1, heads):
        terms.append(shift(moved[step], "head", -step).astype(jnp.float32))
    head = lax.axis_index("head")
    rows = []
    for r in range(row_count):
        total = None
        for step, term in enumerate(terms):
            if row_count > 1:
                source = lax.rem(head - step + heads, heads) // HEAD_COUNT
                term = jnp.where(source == r, term, 0.0)
            total = term if total is None else total + term
        rows.append(total)
    grad_keys = jnp.stack([total[0] for total in rows])
    grad_values = jnp.stack([total[1] for total in rows])
    return grad_queries, grad_keys, grad_values


def solution(mesh):
    in_specs = (
        P("head", "seq", None),
        P(None, "seq", None),
        P(None, "seq", None),
        P("head", "seq", None),
        P(),
        P(),
    )
    out_specs = (
        P("head", "seq", None),
        P(None, ("seq", "head"), None),
        P(None, ("seq", "head"), None),
    )
    return jax.shard_map(
        per_device, mesh=mesh, in_specs=in_specs, out_specs=out_specs, check_vma=False
    )
```

time: 124 us -> 53.7 us (0.43)
  waiting for transfers between devices: 73.8 us -> 9.61 us
  Pallas kernels: 0 us -> 17.4 us
  matrix products: 16.5 us -> 0 us
  between operations: 13.9 us -> 0.68 us
  starting transfers between devices: 11.2 us -> 20.3 us
  other arithmetic: 6.24 us -> 0.84 us
  local copies, waits for them, and re-layouts: 1.69 us -> 4.66 us
    reduce_scatter x2 -> x0, waiting for transfers between devices: 39.6 us -> none  [the longest x1 21.7 us: per_device(): lax.psum_scatter(full_keys.astype(jnp.bfloat16), 'seq', scatter_dimension...]
    all_gather x2 -> x0, waiting for transfers between devices: 27.7 us -> none  [the longest x1 17.1 us: per_device(): key_part = lax.all_gather(key_row, 'seq', axis=0, tiled=True)]
    ppermute x0 -> x16, starting transfers between devices: none -> 20.3 us  [the longest x12 19.2 us: shift(): lax.ppermute(x, axis, [(i, (i - amount) % size) for i in range(size)])]
    pallas_call x0 -> x5, Pallas kernels: none -> 17.4 us  [the longest x2 9.33 us: per_device(): pl.pallas_call(functools.partial(grads_body, offset, factor, chips, first...]
    dot_general x6 -> x0, matrix products: 16.5 us -> none  [the longest x2 4.69 us: contract_first(): lax.dot_general(left, right, (((0,), (0,)), ((), ())), preferred_element_...]
    all_to_all x2 -> x0, starting transfers between devices: 11 us -> none  [the longest x1 5.51 us: owner_blocks(): lax.all_to_all(key_part.astype(jnp.bfloat16), 'head', split_axis=0, conca...]
    ppermute x0 -> x16, waiting for transfers between devices: none -> 9.61 us  [the longest x12 9.22 us: shift(): lax.ppermute(x, axis, [(i, (i - amount) % size) for i in range(size)])]
    all_to_all x2 -> x0, waiting for transfers between devices: 5.07 us -> none  [the longest x1 5.07 us: owner_blocks(): lax.all_to_all(key_part.astype(jnp.bfloat16), 'head', split_axis=0, conca...]
  transfers between devices with their start and end apart: 6 -> 16, of which waited for: 5 -> 6; matrix products, arithmetic and copies ran while one was open for 18% -> 1% of each run, Pallas kernels for 0% -> 22%
where the time goes in v1:
time: 53.7 us; the launch traced here: 53.5 us
  starting transfers between devices  20.3 us (38%)
  Pallas kernels  17.4 us (32%)
  waiting for transfers between devices  9.61 us (18%)
  local copies, waits for them, and re-layouts  4.66 us (9%)
  other arithmetic  0.84 us (2%)
  between operations  0.68 us (1%)
    ppermute x12, starting transfers between devices, shift(): lax.ppermute(x, axis, [(i, (i - amount) % size) for i in range(size)])  19.2 us
    pallas_call x2, Pallas kernels, per_device(): pl.pallas_call(functools.partial(grads_body, offset, factor, chips, first...  9.33 us
    ppermute x12, waiting for transfers between devices, shift(): lax.ppermute(x, axis, [(i, (i - amount) % size) for i in range(size)])  9.22 us
    pallas_call x2, Pallas kernels, per_device(): pl.pallas_call(functools.partial(stats_body, offset, factor), out_shape=j...  5.81 us
    unnamed x22, local copies, waits for them, and re-layouts  4 us
    pallas_call x1, Pallas kernels, per_device(): pl.pallas_call(functools.partial(pieces_body, scaling), out_shape=[jax.Sh...  2.26 us
    ppermute x4, starting transfers between devices, swap_cores(): lax.ppermute(x, 'seq', [(i, i ^ 1) for i in range(lax.axis_size('seq'))])  1.15 us
  transfers between devices with their start and end apart: 16, of which 6 were waited for; matrix products, arithmetic and copies ran while one was open for 1% of the time, Pallas kernels for 22%

profile of v1, /device:TPU:0, one launch (start us, length us, event | category | flops | bytes accessed | tf_op | source)
XLA Modules:
  0.0 53.5 jit_solution(8251429957816247537)
XLA Ops:
  0.6 0.6 %collective-permute-start = (bf16[512,256]{1,0:T(8,128)(2,1)}, bf16[512,256]{1,0:T(8,128)(2,1)S(1)}, u32[]{:S(2)}, u32[]{:S(2)}) collective-permute-start(bf16[512,256]{1,0:T(8,128)(2,1)} %bitcast.12), channel_id=1, source_target_pairs={{0,8},{8,0},{16,24},{24,16},{1,9},{9,1},{17,25},{25,17},{2,10},{10... | collective-permute-start | bytes 786440 | tf_op jit(solution)/shard_map/ppermute | solution.py:187
  1.2 0.1 collective-permute-start.1
  1.3 2.9 %collective-permute-start.2 = (bf16[512,256]{1,0:T(8,128)(2,1)}, bf16[512,256]{1,0:T(8,128)(2,1)S(1)}, u32[]{:S(2)}, u32[]{:S(2)}) collective-permute-start(bf16[512,256]{1,0:T(8,128)(2,1)} %bitcast.6), channel_id=1, source_target_pairs={{0,16},{8,24},{16,0},{24,8},{1,17},{9,25},{17,1},{25,9},{2,18},{10... | collective-permute-start | bytes 786440 | tf_op jit(solution)/shard_map/ppermute | solution.py:183
  4.2 0.0 collective-permute-start.3
  4.2 0.0 collective-permute-done.key_sib.refs_6_
  4.2 0.0 copy-start.5
  4.2 0.0 collective-permute-done.1.value_sib.refs_7_
  4.2 0.7 %copy-done.5 = bf16[512,256]{1,0:T(8,128)(2,1)} copy-done((bf16[512,256]{1,0:T(8,128)(2,1)}, bf16[512,256]{1,0:T(8,128)(2,1)S(1)}, u32[]{:S(2)}) %copy-start.5) | copy-done | bytes 262168
  4.9 0.0 copy-start.6
  4.9 0.7 %copy-done.6 = bf16[512,256]{1,0:T(8,128)(2,1)} copy-done((bf16[512,256]{1,0:T(8,128)(2,1)}, bf16[512,256]{1,0:T(8,128)(2,1)S(1)}, u32[]{:S(2)}) %copy-start.6) | copy-done | bytes 262168
  5.6 3.4 %stats0.1.refs_8_ = f32[3,512]{1,0:T(4,128)} custom-call(s32[1,8]{1,0:T(1,128)} %refs_0_.3, s32[8]{0:T(128)} %refs_1_.3, bf16[512,256]{1,0:T(8,128)(2,1)} %bitcast.7, bf16[512,256]{1,0:T(8,128)(2,1)} %bitcast.10, bf16[512,256]{1,0:T(8,128)(2,1)} %bitcast.13, bf16[512,256]{1,0:T(8,128)(2,1)} %bitcast.18, bf16[512,256]{1,0:T(8,128)(2,1)} %copy-done.5, ...), custom_call_target="tpu_custom_call" | custom-call | flops 536870912 | bytes 1572864 | tf_op jit(solution)/shard_map/stats0/pallas_call | solution.py:216
  9.0 1.3 %collective-permute-start.5 = (f32[3,512]{1,0:T(4,128)}, f32[3,512]{1,0:T(4,128)S(1)}, u32[]{:S(2)}, u32[]{:S(2)}) collective-permute-start(f32[3,512]{1,0:T(4,128)} %stats0.1.refs_8_), channel_id=1, source_target_pairs={{0,16},{8,24},{16,0},{24,8},{1,17},{9,25},{17,1},{25,9},{2,18},{10... | collective-permute-start | bytes 18440 | tf_op jit(solution)/shard_map/ppermute | solution.py:183
  10.4 1.2 %collective-permute-done.2.query.refs_2_ = bf16[512,256]{1,0:T(8,128)(2,1)S(1)} collective-permute-done((bf16[512,256]{1,0:T(8,128)(2,1)}, bf16[512,256]{1,0:T(8,128)(2,1)S(1)}, u32[]{:S(2)}, u32[]{:S(2)}) %collective-permute-start.2) | collective-permute-done | bytes 262176 | tf_op jit(solution)/shard_map/ppermute | solution.py:183
  11.6 0.0 copy-start.7
  11.6 5.1 %collective-permute-done.3.grad.refs_3_ = bf16[512,256]{1,0:T(8,128)(2,1)S(1)} collective-permute-done((bf16[512,256]{1,0:T(8,128)(2,1)}, bf16[512,256]{1,0:T(8,128)(2,1)S(1)}, u32[]{:S(2)}, u32[]{:S(2)}) %collective-permute-start.3) | collective-permute-done | bytes 262176 | tf_op jit(solution)/shard_map/ppermute | solution.py:183
  16.7 0.0 copy-done.7
  16.7 0.0 copy-start.8
  16.7 0.7 %copy-done.8 = bf16[512,256]{1,0:T(8,128)(2,1)} copy-done((bf16[512,256]{1,0:T(8,128)(2,1)}, bf16[512,256]{1,0:T(8,128)(2,1)S(1)}, u32[]{:S(2)}) %copy-start.8) | copy-done | bytes 262168
  17.4 2.4 %stats1.1.refs_8_ = f32[3,512]{1,0:T(4,128)} custom-call(s32[1,8]{1,0:T(1,128)} %refs_0_.3, s32[8]{0:T(128)} %refs_1_.3, bf16[512,256]{1,0:T(8,128)(2,1)} %copy-done.7, bf16[512,256]{1,0:T(8,128)(2,1)} %copy-done.8, bf16[512,256]{1,0:T(8,128)(2,1)} %bitcast.14, bf16[512,256]{1,0:T(8,128)(2,1)} %bitcast.19, bf16[512,256]{1,0:T(8,128)(2,1)} %copy-done.5, ...), custom_call_target="tpu_custom_call" | custom-call | flops 536870912 | bytes 1572864 | tf_op jit(solution)/shard_map/stats1/pallas_call | solution.py:216
  19.8 1.4 %collective-permute-start.4 = (f32[3,512]{1,0:T(4,128)}, f32[3,512]{1,0:T(4,128)S(1)}, u32[]{:S(2)}, u32[]{:S(2)}) collective-permute-start(f32[3,512]{1,0:T(4,128)} %stats1.1.refs_8_), channel_id=1, source_target_pairs={{0,16},{8,24},{16,0},{24,8},{1,17},{9,25},{17,1},{25,9},{2,18},{10... | collective-permute-start | bytes 18440 | tf_op jit(solution)/shard_map/ppermute | solution.py:183
  21.2 0.0 collective-permute-done.5.refs_9_
  21.2 0.0 copy-start.10
  21.2 0.6 %copy-done.10 = f32[3,512]{1,0:T(4,128)} copy-done((f32[3,512]{1,0:T(4,128)}, f32[3,512]{1,0:T(4,128)S(1)}, u32[]{:S(2)}) %copy-start.10) | copy-done | bytes 6168
  21.8 3.6 %grads1.1 = (bf16[512,256]{1,0:T(8,128)(2,1)}, f32[1024,256]{1,0:T(8,128)}, f32[1024,256]{1,0:T(8,128)}) custom-call(s32[1,8]{1,0:T(1,128)} %refs_0_.3, s32[8]{0:T(128)} %refs_1_.3, bf16[512,256]{1,0:T(8,128)(2,1)} %copy-done.7, bf16[512,256]{1,0:T(8,128)(2,1)} %copy-done.8, bf16[512,256]{1,0:T(8,128)(2,1)} %bitcast.15, bf16[512,256]{1,0:T(8,128)(2,1)} %bitcast.20, ...), custom_call_target="tpu_custom_call" | custom-call | flops 1342177280 | bytes 4194304 | tf_op jit(solution)/shard_map/grads1/pallas_call | solution.py:245
  25.4 0.0 collective-permute-done.4.refs_9_
  25.4 0.0 copy-start.9
  25.4 0.6 %copy-done.9 = f32[3,512]{1,0:T(4,128)} copy-done((f32[3,512]{1,0:T(4,128)}, f32[3,512]{1,0:T(4,128)S(1)}, u32[]{:S(2)}) %copy-start.9) | copy-done | bytes 6168
  26.0 0.0 copy-start.4
  26.0 5.7 %grads0.1 = (f32[512,256]{1,0:T(8,128)}, f32[512,256]{1,0:T(8,128)}, f32[512,256]{1,0:T(8,128)}, bf16[512,256]{1,0:T(8,128)(2,1)}, bf16[512,256]{1,0:T(8,128)(2,1)}) custom-call(s32[1,8]{1,0:T(1,128)} %refs_0_.3, s32[8]{0:T(128)} %refs_1_.3, bf16[512,256]{1,0:T(8,128)(2,1)} %bitcast.8, bf16[512,256]{1,0:T(8,128)(2,1)} %bitcast.11, ...), custom_call_target="tpu_custom_call" | custom-call | flops 1342177280 | bytes 4194304 | tf_op jit(solution)/shard_map/grads0/pallas_call | solution.py:245
  31.7 0.0 collective-permute-start.7
  31.7 0.5 collective-permute-start.8
  32.2 0.0 copy-done.4
  32.2 1.2 %collective-permute-start.6 = (bf16[512,256]{1,0:T(8,128)(2,1)S(1)}, bf16[512,256]{1,0:T(8,128)(2,1)S(1)}, u32[]{:S(2)}, u32[]{:S(2)}) collective-permute-start(bf16[512,256]{1,0:T(8,128)(2,1)S(1)} %copy-done.4), channel_id=1, source_target_pairs={{0,16},{8,24},{16,0},{24,8},{1,17},{9,25},{17,1},{25,9},{2,18},{10... | collective-permute-start | bytes 786440 | tf_op jit(solution)/shard_map/ppermute | solution.py:183
  33.5 0.0 collective-permute-done.7.dk_in
  33.5 0.0 copy-start.1
  33.5 0.4 collective-permute-done.8.dv_in
  33.8 0.0 copy-start.2
  33.8 0.3 copy-done.1
  34.2 0.4 copy-done.2
  34.5 0.0 copy-start
  34.5 2.3 %pieces.1 = (f32[2,64,256]{2,1,0:T(8,128)}, bf16[2,64,256]{2,1,0:T(8,128)(2,1)}, bf16[2,64,256]{2,1,0:T(8,128)(2,1)}, bf16[2,64,256]{2,1,0:T(8,128)(2,1)}, bf16[...) custom-call(f32[512,256]{1,0:T(8,128)} %get-tuple-element.23.dk, ...), custom_call_target="tpu_custom_call" | custom-call | flops 524288 | bytes 4194304 | tf_op jit(solution)/shard_map/pieces/pallas_call | solution.py:271
  36.8 1.5 %collective-permute-start.9 = (bf16[2,64,256]{2,1,0:T(8,128)(2,1)}, bf16[2,64,256]{2,1,0:T(8,128)(2,1)S(1)}, u32[]{:S(2)}, u32[]{:S(2)}) collective-permute-start(bf16[2,64,256]{2,1,0:T(8,128)(2,1)} %get-tuple-element.28), channel_id=1, source_target_pairs={{0,1},{1,2},{2,3},{3,4},{4,5},{5,6},{6,7},{7,0},{8,9},{9,10},{10,1... | collective-permute-start | bytes 196616 | tf_op jit(solution)/shard_map/ppermute | solution.py:183
  38.3 1.6 %collective-permute-start.10 = (bf16[2,64,256]{2,1,0:T(8,128)(2,1)}, bf16[2,64,256]{2,1,0:T(8,128)(2,1)S(1)}, u32[]{:S(2)}, u32[]{:S(2)}) collective-permute-start(bf16[2,64,256]{2,1,0:T(8,128)(2,1)} %get-tuple-element.29), channel_id=1, source_target_pairs={{0,2},{1,3},{2,4},{3,5},{4,6},{5,7},{6,0},{7,1},{8,10},{9,11},{10,... | collective-permute-start | bytes 196616 | tf_op jit(solution)/shard_map/ppermute | solution.py:183
  39.9 2.6 %collective-permute-start.11 = (bf16[2,64,256]{2,1,0:T(8,128)(2,1)}, bf16[2,64,256]{2,1,0:T(8,128)(2,1)S(1)}, u32[]{:S(2)}, u32[]{:S(2)}) collective-permute-start(bf16[2,64,256]{2,1,0:T(8,128)(2,1)} %get-tuple-element.30), channel_id=1, source_target_pairs={{0,3},{1,4},{2,5},{3,6},{4,7},{5,0},{6,1},{7,2},{8,11},{9,12},{10,... | collective-permute-start | bytes 196616 | tf_op jit(solution)/shard_map/ppermute | solution.py:183
  42.4 1.2 %collective-permute-start.12 = (bf16[2,64,256]{2,1,0:T(8,128)(2,1)}, bf16[2,64,256]{2,1,0:T(8,128)(2,1)S(1)}, u32[]{:S(2)}, u32[]{:S(2)}) collective-permute-start(bf16[2,64,256]{2,1,0:T(8,128)(2,1)} %get-tuple-element.31), channel_id=1, source_target_pairs={{0,4},{1,5},{2,6},{3,7},{4,0},{5,1},{6,2},{7,3},{8,12},{9,13},{10,... | collective-permute-start | bytes 196616 | tf_op jit(solution)/shard_map/ppermute | solution.py:183
  43.7 0.0 collective-permute-done.6
  43.7 2.6 %collective-permute-start.13 = (bf16[2,64,256]{2,1,0:T(8,128)(2,1)}, bf16[2,64,256]{2,1,0:T(8,128)(2,1)S(1)}, u32[]{:S(2)}, u32[]{:S(2)}) collective-permute-start(bf16[2,64,256]{2,1,0:T(8,128)(2,1)} %get-tuple-element.32), channel_id=1, source_target_pairs={{0,5},{1,6},{2,7},{3,0},{4,1},{5,2},{6,3},{7,4},{8,13},{9,14},{10,... | collective-permute-start | bytes 196616 | tf_op jit(solution)/shard_map/ppermute | solution.py:183
  46.3 0.0 collective-permute-done.9
  46.3 1.3 %collective-permute-start.14 = (bf16[2,64,256]{2,1,0:T(8,128)(2,1)}, bf16[2,64,256]{2,1,0:T(8,128)(2,1)S(1)}, u32[]{:S(2)}, u32[]{:S(2)}) collective-permute-start(bf16[2,64,256]{2,1,0:T(8,128)(2,1)} %get-tuple-element.33), channel_id=1, source_target_pairs={{0,6},{1,7},{2,0},{3,1},{4,2},{5,3},{6,4},{7,5},{8,14},{9,15},{10,... | collective-permute-start | bytes 196616 | tf_op jit(solution)/shard_map/ppermute | solution.py:183
  47.6 0.0 collective-permute-done.10
  47.7 1.4 %collective-permute-start.15 = (bf16[2,64,256]{2,1,0:T(8,128)(2,1)}, bf16[2,64,256]{2,1,0:T(8,128)(2,1)S(1)}, u32[]{:S(2)}, u32[]{:S(2)}) collective-permute-start(bf16[2,64,256]{2,1,0:T(8,128)(2,1)} %get-tuple-element.34), channel_id=1, source_target_pairs={{0,7},{1,0},{2,1},{3,2},{4,3},{5,4},{6,5},{7,6},{8,15},{9,8},{10,9... | collective-permute-start | bytes 196616 | tf_op jit(solution)/shard_map/ppermute | solution.py:183
  49.1 0.0 copy-done
  49.1 0.0 copy-start.3
  49.1 0.8 %fusion = bf16[1,512,256]{2,1,0:T(8,128)(2,1)} fusion(f32[512,256]{1,0:T(8,128)S(1)} %copy-done, bf16[512,256]{1,0:T(8,128)(2,1)S(1)} %collective-permute-done.6), kind=kLoop, calls=%fused_computation.1 | loop fusion | flops 524288 | bytes 1048576 | tf_op jit(solution)/shard_map/broadcast_in_dim | solution.py:269
  49.9 0.0 collective-permute-done.11
  49.9 0.8 %collective-permute-done.12 = bf16[2,64,256]{2,1,0:T(8,128)(2,1)S(1)} collective-permute-done((bf16[2,64,256]{2,1,0:T(8,128)(2,1)}, bf16[2,64,256]{2,1,0:T(8,128)(2,1)S(1)}, u32[]{:S(2)}, u32[]{:S(2)}) %collective-permute-start.12) | collective-permute-done | bytes 65568 | tf_op jit(solution)/shard_map/ppermute | solution.py:183
  50.7 0.9 %collective-permute-done.13 = bf16[2,64,256]{2,1,0:T(8,128)(2,1)S(1)} collective-permute-done((bf16[2,64,256]{2,1,0:T(8,128)(2,1)}, bf16[2,64,256]{2,1,0:T(8,128)(2,1)S(1)}, u32[]{:S(2)}, u32[]{:S(2)}) %collective-permute-start.13) | collective-permute-done | bytes 65568 | tf_op jit(solution)/shard_map/ppermute | solution.py:183
  51.6 1.1 %collective-permute-done.14 = bf16[2,64,256]{2,1,0:T(8,128)(2,1)S(1)} collective-permute-done((bf16[2,64,256]{2,1,0:T(8,128)(2,1)}, bf16[2,64,256]{2,1,0:T(8,128)(2,1)S(1)}, u32[]{:S(2)}, u32[]{:S(2)}) %collective-permute-start.14) | collective-permute-done | bytes 65568 | tf_op jit(solution)/shard_map/ppermute | solution.py:183
  52.8 0.0 collective-permute-done.15
  52.8 0.0 copy-done.3
  52.8 0.1 convert_add_fusion
  52.9 0.7 %fusion.1 = (f32[1,64,256]{2,1,0:T(8,128)}, f32[1,64,256]{2,1,0:T(8,128)}) fusion(f32[2,64,256]{2,1,0:T(8,128)S(1)} %convert_add_fusion), kind=kLoop, calls=%fused_computation.3 | loop fusion | bytes 262144 | tf_op jit(solution)/shard_map/slice | solution.py:296
Async XLA Ops:
  0.6 3.6 %collective-permute-start = (bf16[512,256]{1,0:T(8,128)(2,1)}, bf16[512,256]{1,0:T(8,128)(2,1)S(1)}, u32[]{:S(2)}, u32[]{:S(2)}) collective-permute-start(bf16[512,256]{1,0:T(8,128)(2,1)} %bitcast.12), channel_id=1, source_target_pairs={{0,8},{8,0},{16,24},{24,16},{1,9},{9,1},{17,25},{25,17},{2,10},{10... | collective-permute-start | bytes 786440 | tf_op jit(solution)/shard_map/ppermute | solution.py:187
  1.2 3.0 %collective-permute-start.1 = (bf16[512,256]{1,0:T(8,128)(2,1)}, bf16[512,256]{1,0:T(8,128)(2,1)S(1)}, u32[]{:S(2)}, u32[]{:S(2)}) collective-permute-start(bf16[512,256]{1,0:T(8,128)(2,1)} %bitcast.17), channel_id=1, source_target_pairs={{0,8},{8,0},{16,24},{24,16},{1,9},{9,1},{17,25},{25,17},{2,10},{10... | collective-permute-start | bytes 786440 | tf_op jit(solution)/shard_map/ppermute | solution.py:187
  1.3 10.3 %collective-permute-start.2 = (bf16[512,256]{1,0:T(8,128)(2,1)}, bf16[512,256]{1,0:T(8,128)(2,1)S(1)}, u32[]{:S(2)}, u32[]{:S(2)}) collective-permute-start(bf16[512,256]{1,0:T(8,128)(2,1)} %bitcast.6), channel_id=1, source_target_pairs={{0,16},{8,24},{16,0},{24,8},{1,17},{9,25},{17,1},{25,9},{2,18},{10... | collective-permute-start | bytes 786440 | tf_op jit(solution)/shard_map/ppermute | solution.py:183
  4.2 12.5 %collective-permute-start.3 = (bf16[512,256]{1,0:T(8,128)(2,1)}, bf16[512,256]{1,0:T(8,128)(2,1)S(1)}, u32[]{:S(2)}, u32[]{:S(2)}) collective-permute-start(bf16[512,256]{1,0:T(8,128)(2,1)} %bitcast.9), channel_id=1, source_target_pairs={{0,16},{8,24},{16,0},{24,8},{1,17},{9,25},{17,1},{25,9},{2,18},{10... | collective-permute-start | bytes 786440 | tf_op jit(solution)/shard_map/ppermute | solution.py:183
  4.2 0.7 %copy-start.5 = (bf16[512,256]{1,0:T(8,128)(2,1)}, bf16[512,256]{1,0:T(8,128)(2,1)S(1)}, u32[]{:S(2)}) copy-start(bf16[512,256]{1,0:T(8,128)(2,1)S(1)} %collective-permute-done.key_sib.refs_6_) | copy-start | bytes 786436
  4.9 0.7 %copy-start.6 = (bf16[512,256]{1,0:T(8,128)(2,1)}, bf16[512,256]{1,0:T(8,128)(2,1)S(1)}, u32[]{:S(2)}) copy-start(bf16[512,256]{1,0:T(8,128)(2,1)S(1)} %collective-permute-done.1.value_sib.refs_7_) | copy-start | bytes 786436
  9.0 12.2 %collective-permute-start.5 = (f32[3,512]{1,0:T(4,128)}, f32[3,512]{1,0:T(4,128)S(1)}, u32[]{:S(2)}, u32[]{:S(2)}) collective-permute-start(f32[3,512]{1,0:T(4,128)} %stats0.1.refs_8_), channel_id=1, source_target_pairs={{0,16},{8,24},{16,0},{24,8},{1,17},{9,25},{17,1},{25,9},{2,18},{10... | collective-permute-start | bytes 18440 | tf_op jit(solution)/shard_map/ppermute | solution.py:183
  11.6 5.1 %copy-start.7 = (bf16[512,256]{1,0:T(8,128)(2,1)}, bf16[512,256]{1,0:T(8,128)(2,1)S(1)}, u32[]{:S(2)}) copy-start(bf16[512,256]{1,0:T(8,128)(2,1)S(1)} %collective-permute-done.2.query.refs_2_) | copy-start | bytes 786436
  16.7 0.7 %copy-start.8 = (bf16[512,256]{1,0:T(8,128)(2,1)}, bf16[512,256]{1,0:T(8,128)(2,1)S(1)}, u32[]{:S(2)}) copy-start(bf16[512,256]{1,0:T(8,128)(2,1)S(1)} %collective-permute-done.3.grad.refs_3_) | copy-start | bytes 786436
  19.8 5.6 %collective-permute-start.4 = (f32[3,512]{1,0:T(4,128)}, f32[3,512]{1,0:T(4,128)S(1)}, u32[]{:S(2)}, u32[]{:S(2)}) collective-permute-start(f32[3,512]{1,0:T(4,128)} %stats1.1.refs_8_), channel_id=1, source_target_pairs={{0,16},{8,24},{16,0},{24,8},{1,17},{9,25},{17,1},{25,9},{2,18},{10... | collective-permute-start | bytes 18440 | tf_op jit(solution)/shard_map/ppermute | solution.py:183
  21.2 0.6 %copy-start.10 = (f32[3,512]{1,0:T(4,128)}, f32[3,512]{1,0:T(4,128)S(1)}, u32[]{:S(2)}) copy-start(f32[3,512]{1,0:T(4,128)S(1)} %collective-permute-done.5.refs_9_) | copy-start | bytes 18436
  25.4 0.6 %copy-start.9 = (f32[3,512]{1,0:T(4,128)}, f32[3,512]{1,0:T(4,128)S(1)}, u32[]{:S(2)}) copy-start(f32[3,512]{1,0:T(4,128)S(1)} %collective-permute-done.4.refs_9_) | copy-start | bytes 18436
  26.0 6.2 %copy-start.4 = (bf16[512,256]{1,0:T(8,128)(2,1)S(1)}, bf16[512,256]{1,0:T(8,128)(2,1)}, u32[]{:S(2)}) copy-start(bf16[512,256]{1,0:T(8,128)(2,1)} %get-tuple-element.22) | copy-start | bytes 786436
  31.7 1.7 %collective-permute-start.7 = (bf16[512,256]{1,0:T(8,128)(2,1)}, bf16[512,256]{1,0:T(8,128)(2,1)S(1)}, u32[]{:S(2)}, u32[]{:S(2)}) collective-permute-start(bf16[512,256]{1,0:T(8,128)(2,1)} %get-tuple-element.25), channel_id=1, source_target_pairs={{0,8},{8,0},{16,24},{24,16},{1,9},{9,1},{17,25},{25,17},{2,10},{10... | collective-permute-start | bytes 786440 | tf_op jit(solution)/shard_map/ppermute | solution.py:187
  31.7 2.1 %collective-permute-start.8 = (bf16[512,256]{1,0:T(8,128)(2,1)}, bf16[512,256]{1,0:T(8,128)(2,1)S(1)}, u32[]{:S(2)}, u32[]{:S(2)}) collective-permute-start(bf16[512,256]{1,0:T(8,128)(2,1)} %get-tuple-element.26), channel_id=1, source_target_pairs={{0,8},{8,0},{16,24},{24,16},{1,9},{9,1},{17,25},{25,17},{2,10},{10... | collective-permute-start | bytes 786440 | tf_op jit(solution)/shard_map/ppermute | solution.py:187
  32.2 11.4 %collective-permute-start.6 = (bf16[512,256]{1,0:T(8,128)(2,1)S(1)}, bf16[512,256]{1,0:T(8,128)(2,1)S(1)}, u32[]{:S(2)}, u32[]{:S(2)}) collective-permute-start(bf16[512,256]{1,0:T(8,128)(2,1)S(1)} %copy-done.4), channel_id=1, source_target_pairs={{0,16},{8,24},{16,0},{24,8},{1,17},{9,25},{17,1},{25,9},{2,18},{10... | collective-permute-start | bytes 786440 | tf_op jit(solution)/shard_map/ppermute | solution.py:183
  33.5 0.7 %copy-start.1 = (bf16[512,256]{1,0:T(8,128)(2,1)}, bf16[512,256]{1,0:T(8,128)(2,1)S(1)}, u32[]{:S(2)}) copy-start(bf16[512,256]{1,0:T(8,128)(2,1)S(1)} %collective-permute-done.7.dk_in) | copy-start | bytes 786436
  33.8 0.7 %copy-start.2 = (bf16[512,256]{1,0:T(8,128)(2,1)}, bf16[512,256]{1,0:T(8,128)(2,1)S(1)}, u32[]{:S(2)}) copy-start(bf16[512,256]{1,0:T(8,128)(2,1)S(1)} %collective-permute-done.8.dv_in) | copy-start | bytes 786436
  34.5 14.5 %copy-start = (f32[512,256]{1,0:T(8,128)S(1)}, f32[512,256]{1,0:T(8,128)}, u32[]{:S(2)}) copy-start(f32[512,256]{1,0:T(8,128)} %get-tuple-element.21) | copy-start | bytes 1572868
  36.8 9.5 %collective-permute-start.9 = (bf16[2,64,256]{2,1,0:T(8,128)(2,1)}, bf16[2,64,256]{2,1,0:T(8,128)(2,1)S(1)}, u32[]{:S(2)}, u32[]{:S(2)}) collective-permute-start(bf16[2,64,256]{2,1,0:T(8,128)(2,1)} %get-tuple-element.28), channel_id=1, source_target_pairs={{0,1},{1,2},{2,3},{3,4},{4,5},{5,6},{6,7},{7,0},{8,9},{9,10},{10,1... | collective-permute-start | bytes 196616 | tf_op jit(solution)/shard_map/ppermute | solution.py:183
  38.3 9.4 %collective-permute-start.10 = (bf16[2,64,256]{2,1,0:T(8,128)(2,1)}, bf16[2,64,256]{2,1,0:T(8,128)(2,1)S(1)}, u32[]{:S(2)}, u32[]{:S(2)}) collective-permute-start(bf16[2,64,256]{2,1,0:T(8,128)(2,1)} %get-tuple-element.29), channel_id=1, source_target_pairs={{0,2},{1,3},{2,4},{3,5},{4,6},{5,7},{6,0},{7,1},{8,10},{9,11},{10,... | collective-permute-start | bytes 196616 | tf_op jit(solution)/shard_map/ppermute | solution.py:183
  39.9 10.0 %collective-permute-start.11 = (bf16[2,64,256]{2,1,0:T(8,128)(2,1)}, bf16[2,64,256]{2,1,0:T(8,128)(2,1)S(1)}, u32[]{:S(2)}, u32[]{:S(2)}) collective-permute-start(bf16[2,64,256]{2,1,0:T(8,128)(2,1)} %get-tuple-element.30), channel_id=1, source_target_pairs={{0,3},{1,4},{2,5},{3,6},{4,7},{5,0},{6,1},{7,2},{8,11},{9,12},{10,... | collective-permute-start | bytes 196616 | tf_op jit(solution)/shard_map/ppermute | solution.py:183
  42.4 8.2 %collective-permute-start.12 = (bf16[2,64,256]{2,1,0:T(8,128)(2,1)}, bf16[2,64,256]{2,1,0:T(8,128)(2,1)S(1)}, u32[]{:S(2)}, u32[]{:S(2)}) collective-permute-start(bf16[2,64,256]{2,1,0:T(8,128)(2,1)} %get-tuple-element.31), channel_id=1, source_target_pairs={{0,4},{1,5},{2,6},{3,7},{4,0},{5,1},{6,2},{7,3},{8,12},{9,13},{10,... | collective-permute-start | bytes 196616 | tf_op jit(solution)/shard_map/ppermute | solution.py:183
  43.7 7.9 %collective-permute-start.13 = (bf16[2,64,256]{2,1,0:T(8,128)(2,1)}, bf16[2,64,256]{2,1,0:T(8,128)(2,1)S(1)}, u32[]{:S(2)}, u32[]{:S(2)}) collective-permute-start(bf16[2,64,256]{2,1,0:T(8,128)(2,1)} %get-tuple-element.32), channel_id=1, source_target_pairs={{0,5},{1,6},{2,7},{3,0},{4,1},{5,2},{6,3},{7,4},{8,13},{9,14},{10,... | collective-permute-start | bytes 196616 | tf_op jit(solution)/shard_map/ppermute | solution.py:183
  46.3 6.5 %collective-permute-start.14 = (bf16[2,64,256]{2,1,0:T(8,128)(2,1)}, bf16[2,64,256]{2,1,0:T(8,128)(2,1)S(1)}, u32[]{:S(2)}, u32[]{:S(2)}) collective-permute-start(bf16[2,64,256]{2,1,0:T(8,128)(2,1)} %get-tuple-element.33), channel_id=1, source_target_pairs={{0,6},{1,7},{2,0},{3,1},{4,2},{5,3},{6,4},{7,5},{8,14},{9,15},{10,... | collective-permute-start | bytes 196616 | tf_op jit(solution)/shard_map/ppermute | solution.py:183
  47.7 5.1 %collective-permute-start.15 = (bf16[2,64,256]{2,1,0:T(8,128)(2,1)}, bf16[2,64,256]{2,1,0:T(8,128)(2,1)S(1)}, u32[]{:S(2)}, u32[]{:S(2)}) collective-permute-start(bf16[2,64,256]{2,1,0:T(8,128)(2,1)} %get-tuple-element.34), channel_id=1, source_target_pairs={{0,7},{1,0},{2,1},{3,2},{4,3},{5,4},{6,5},{7,6},{8,15},{9,8},{10,9... | collective-permute-start | bytes 196616 | tf_op jit(solution)/shard_map/ppermute | solution.py:183
  49.1 3.7 %copy-start.3 = (f32[2,64,256]{2,1,0:T(8,128)S(1)}, f32[2,64,256]{2,1,0:T(8,128)}, u32[]{:S(2)}) copy-start(f32[2,64,256]{2,1,0:T(8,128)} %get-tuple-element.27) | copy-start | bytes 393220

commit v2 on v1

--- a/solution.py
+++ b/solution.py
@@ -10,6 +10,7 @@
 
 HEAD_COUNT = 8
 MASKED = -1e30
+VMEM_LIMIT = 14 * 1024 * 1024
 CORES = 2
 
 
@@ -219,6 +220,7 @@
                 in_specs=[SMEM] * 2 + [VMEM] * 6,
                 out_specs=VMEM,
                 name=f"stats{offset}",
+                compiler_params=pltpu.CompilerParams(vmem_limit_bytes=VMEM_LIMIT),
                 cost_estimate=pl.CostEstimate(
                     flops=4 * tiles, bytes_accessed=6 * local * width * 2, transcendentals=0
                 ),
@@ -253,7 +255,8 @@
                 pltpu.VMEM((local, width), jnp.float32),
             ],
             name=f"grads{offset}",
-            cost_estimate=pl.CostEstimate(
+            compiler_params=pltpu.CompilerParams(vmem_limit_bytes=VMEM_LIMIT),
+                cost_estimate=pl.CostEstimate(
                 flops=10 * tiles, bytes_accessed=8 * local * width * 4, transcendentals=0
             ),
         )(*operands)
@@ -275,7 +278,8 @@
         in_specs=[VMEM] * 4,
         out_specs=[VMEM] * heads,
         name="pieces",
-        cost_estimate=pl.CostEstimate(
+        compiler_params=pltpu.CompilerParams(vmem_limit_bytes=VMEM_LIMIT),
+                cost_estimate=pl.CostEstimate(
             flops=4 * local * width, bytes_accessed=8 * local * width * 4, transcendentals=0
         ),
     )(dk, dv, dk_in, dv_in)

time: 53.7 us -> 43.6 us (0.81)
  Pallas kernels: 17.4 us -> 5.85 us
  starting transfers between devices: 20.3 us -> 23 us
  waiting for transfers between devices: 9.61 us -> 8.22 us
    pallas_call x2, Pallas kernels: 9.33 us -> 3.41 us  [per_device(): pl.pallas_call(functools.partial(grads_body, offset, factor, chips, first...]
    pallas_call x2, Pallas kernels: 5.81 us -> 2.32 us  [per_device(): pl.pallas_call(functools.partial(stats_body, offset, factor), out_shape=j...]
    ppermute x12, starting transfers between devices: 19.2 us -> 21.8 us  [shift(): lax.ppermute(x, axis, [(i, (i - amount) % size) for i in range(size)])]
    pallas_call x1, Pallas kernels: 2.26 us -> 0.12 us  [per_device(): pl.pallas_call(functools.partial(pieces_body, scaling), out_shape=[jax.Sh...]
    ppermute x12, waiting for transfers between devices: 9.22 us -> 8.21 us  [shift(): lax.ppermute(x, axis, [(i, (i - amount) % size) for i in range(size)])]
    unnamed x22 -> x20, local copies, waits for them, and re-layouts: 4 us -> 3.84 us
  transfers between devices with their start and end apart: 16 -> 16, of which waited for: 6 -> 4; matrix products, arithmetic and copies ran while one was open for 1% -> 2% of each run, Pallas kernels for 22% -> 8%
where the time goes in v2:
time: 43.6 us; the launch traced here: 43.2 us
  starting transfers between devices  23 us (53%)
  waiting for transfers between devices  8.22 us (19%)
  Pallas kernels  5.85 us (13%)
  local copies, waits for them, and re-layouts  4.5 us (10%)
  other arithmetic  0.84 us (2%)
  between operations  0.74 us (2%)
    ppermute x12, starting transfers between devices, shift(): lax.ppermute(x, axis, [(i, (i - amount) % size) for i in range(size)])  21.8 us
    ppermute x12, waiting for transfers between devices, shift(): lax.ppermute(x, axis, [(i, (i - amount) % size) for i in range(size)])  8.21 us
    unnamed x20, local copies, waits for them, and re-layouts  3.84 us
    pallas_call x2, Pallas kernels, per_device(): pl.pallas_call(functools.partial(grads_body, offset, factor, chips, first...  3.41 us
    pallas_call x2, Pallas kernels, per_device(): pl.pallas_call(functools.partial(stats_body, offset, factor), out_shape=j...  2.32 us
    ppermute x4, starting transfers between devices, swap_cores(): lax.ppermute(x, 'seq', [(i, i ^ 1) for i in range(lax.axis_size('seq'))])  1.2 us
  transfers between devices with their start and end apart: 16, of which 4 were waited for; matrix products, arithmetic and copies ran while one was open for 2% of the time, Pallas kernels for 8%

profile of v2, /device:TPU:0, one launch (start us, length us, event | category | flops | bytes accessed | tf_op | source)
XLA Modules:
  0.0 43.2 jit_solution(16917698034366969386)
XLA Ops:
  0.6 0.6 %collective-permute-start = (bf16[512,256]{1,0:T(8,128)(2,1)}, bf16[512,256]{1,0:T(8,128)(2,1)S(1)}, u32[]{:S(2)}, u32[]{:S(2)}) collective-permute-start(bf16[512,256]{1,0:T(8,128)(2,1)} %bitcast.12), channel_id=1, source_target_pairs={{0,8},{8,0},{16,24},{24,16},{1,9},{9,1},{17,25},{25,17},{2,10},{10... | collective-permute-start | bytes 786440 | tf_op jit(solution)/shard_map/ppermute | solution.py:188
  1.2 0.1 collective-permute-start.1
  1.3 0.0 copy-start.8
  1.3 0.0 copy-start.9
  1.3 2.9 %collective-permute-start.2 = (bf16[512,256]{1,0:T(8,128)(2,1)}, bf16[512,256]{1,0:T(8,128)(2,1)S(1)}, u32[]{:S(2)}, u32[]{:S(2)}) collective-permute-start(bf16[512,256]{1,0:T(8,128)(2,1)} %bitcast.6), channel_id=1, source_target_pairs={{0,16},{8,24},{16,0},{24,8},{1,17},{9,25},{17,1},{25,9},{2,18},{10... | collective-permute-start | bytes 786440 | tf_op jit(solution)/shard_map/ppermute | solution.py:184
  4.2 0.0 collective-permute-start.3
  4.2 0.0 collective-permute-done.key_sib.refs_6_
  4.2 0.0 collective-permute-done.1.value_sib.refs_7_
  4.2 0.0 copy-done.8
  4.2 0.0 copy-done.9
  4.3 0.0 copy-start
  4.3 1.0 %copy-done = bf16[1,512,256]{2,1,0:T(8,128)(2,1)S(1)} copy-done((bf16[1,512,256]{2,1,0:T(8,128)(2,1)S(1)}, bf16[1,512,256]{2,1,0:T(8,128)(2,1)}, u32[]{:S(2)}) %copy-start) | copy-done | bytes 262168
  5.2 0.0 copy-start.2
  5.2 0.9 %copy-done.2 = bf16[1,512,256]{2,1,0:T(8,128)(2,1)S(1)} copy-done((bf16[1,512,256]{2,1,0:T(8,128)(2,1)S(1)}, bf16[1,512,256]{2,1,0:T(8,128)(2,1)}, u32[]{:S(2)}) %copy-start.2) | copy-done | bytes 262168
  6.2 0.0 copy-start.4
  6.2 0.9 %copy-done.4 = bf16[1,512,256]{2,1,0:T(8,128)(2,1)S(1)} copy-done((bf16[1,512,256]{2,1,0:T(8,128)(2,1)S(1)}, bf16[1,512,256]{2,1,0:T(8,128)(2,1)}, u32[]{:S(2)}) %copy-start.4) | copy-done | bytes 262168
  7.1 0.0 copy-start.6
  7.1 0.9 %copy-done.6 = bf16[1,512,256]{2,1,0:T(8,128)(2,1)S(1)} copy-done((bf16[1,512,256]{2,1,0:T(8,128)(2,1)S(1)}, bf16[1,512,256]{2,1,0:T(8,128)(2,1)}, u32[]{:S(2)}) %copy-start.6) | copy-done | bytes 262168
  8.1 0.0 copy-start.5
  8.1 0.0 copy-start.7
  8.1 1.7 %stats0.1.refs_8_ = f32[3,512]{1,0:T(4,128)S(1)} custom-call(s32[1,8]{1,0:T(1,128)S(1)} %copy-done.8, s32[8]{0:T(128)S(1)} %copy-done.9, bf16[512,256]{1,0:T(8,128)(2,1)S(1)} %bitcast.7, bf16[512,256]{1,0:T(8,128)(2,1)S(1)} %bitcast.10, bf16[512,256]{1,0:T(8,128)(2,1)S(1)} %bitcast.13, bf16[512,256]{1,0:T(8,128)(2,1)S(1)} %bitcast.18, ...), custom_call_target="tpu_custom_call" | custom-call | flops 536870912 | bytes 1572864 | tf_op jit(solution)/shard_map/stats0/pallas_call | solution.py:217
  9.8 2.0 %collective-permute-start.5 = (f32[3,512]{1,0:T(4,128)S(1)}, f32[3,512]{1,0:T(4,128)S(1)}, u32[]{:S(2)}, u32[]{:S(2)}) collective-permute-start(f32[3,512]{1,0:T(4,128)S(1)} %stats0.1.refs_8_), channel_id=1, source_target_pairs={{0,16},{8,24},{16,0},{24,8},{1,17},{9,25},{17,1},{25,9},{2,18},{10... | collective-permute-start | bytes 18440 | tf_op jit(solution)/shard_map/ppermute | solution.py:184
  11.8 0.0 collective-permute-done.2.query.refs_2_
  11.8 4.9 %collective-permute-done.3.grad.refs_3_ = bf16[512,256]{1,0:T(8,128)(2,1)S(1)} collective-permute-done((bf16[512,256]{1,0:T(8,128)(2,1)}, bf16[512,256]{1,0:T(8,128)(2,1)S(1)}, u32[]{:S(2)}, u32[]{:S(2)}) %collective-permute-start.3) | collective-permute-done | bytes 262176 | tf_op jit(solution)/shard_map/ppermute | solution.py:184
  16.7 0.0 copy-done.5
  16.7 0.0 copy-done.7
  16.7 0.7 %stats1.1.refs_8_ = f32[3,512]{1,0:T(4,128)S(1)} custom-call(s32[1,8]{1,0:T(1,128)S(1)} %copy-done.8, s32[8]{0:T(128)S(1)} %copy-done.9, bf16[512,256]{1,0:T(8,128)(2,1)S(1)} %collective-permute-done.2.query.refs_2_, bf16[512,256]{1,0:T(8,128)(2,1)S(1)} %collective-permute-done.3.grad.refs_3_, bf16[512,256]{1,0:T(8,128)(2,1)S(1)} %bitcast.14, ...), custom_call_target="tpu_custom_call" | custom-call | flops 536870912 | bytes 1572864 | tf_op jit(solution)/shard_map/stats1/pallas_call | solution.py:217
  17.3 0.0 copy-start.1
  17.3 0.0 copy-start.3
  17.4 2.5 %collective-permute-start.4 = (f32[3,512]{1,0:T(4,128)S(1)}, f32[3,512]{1,0:T(4,128)S(1)}, u32[]{:S(2)}, u32[]{:S(2)}) collective-permute-start(f32[3,512]{1,0:T(4,128)S(1)} %stats1.1.refs_8_), channel_id=1, source_target_pairs={{0,16},{8,24},{16,0},{24,8},{1,17},{9,25},{17,1},{25,9},{2,18},{10... | collective-permute-start | bytes 18440 | tf_op jit(solution)/shard_map/ppermute | solution.py:184
  19.8 0.0 collective-permute-done.5.refs_9_
  19.8 1.0 %grads1.1 = (bf16[512,256]{1,0:T(8,128)(2,1)S(1)}, f32[1024,256]{1,0:T(8,128)S(1)}, f32[1024,256]{1,0:T(8,128)S(1)}) custom-call(s32[1,8]{1,0:T(1,128)S(1)} %copy-done.8, s32[8]{0:T(128)S(1)} %copy-done.9, bf16[512,256]{1,0:T(8,128)(2,1)S(1)} %collective-permute-done.2.query.refs_2_, bf16[512,256]{1,0:T(8,128)(2,1)S(1)} %collective-permute-done.3.grad.refs_3_, ...), custom_call_target="tpu_custom_call" | custom-call | flops 1342177280 | bytes 4194304 | tf_op jit(solution)/shard_map/grads1/pallas_call | solution.py:247
  20.8 0.7 %collective-permute-done.4.refs_9_ = f32[3,512]{1,0:T(4,128)S(1)} collective-permute-done((f32[3,512]{1,0:T(4,128)S(1)}, f32[3,512]{1,0:T(4,128)S(1)}, u32[]{:S(2)}, u32[]{:S(2)}) %collective-permute-start.4) | collective-permute-done | bytes 6176 | tf_op jit(solution)/shard_map/ppermute | solution.py:184
  21.5 0.0 copy-done.1
  21.5 0.0 copy-done.3
  21.5 2.5 %grads0.1 = (f32[512,256]{1,0:T(8,128)S(1)}, f32[512,256]{1,0:T(8,128)S(1)}, f32[512,256]{1,0:T(8,128)S(1)}, bf16[512,256]{1,0:T(8,128)(2,1)S(1)}, bf16[512,256]{1,0:T(8,128)(2,1)S(1)}) custom-call(s32[1,8]{1,0:T(1,128)S(1)} %copy-done.8, s32[8]{0:T(128)S(1)} %copy-done.9, bf16[512,256]{1,0:T(8,128)(2,1)S(1)} %bitcast.8, bf16[512,256]{1,0:T(8,128)(2,1)S(1)} %bitcast.11, ...), custom_call_target="tpu_custom_call" | custom-call | flops 1342177280 | bytes 4194304 | tf_op jit(solution)/shard_map/grads0/pallas_call | solution.py:247
  23.9 0.1 collective-permute-start.7
  24.0 0.5 %collective-permute-start.8 = (bf16[512,256]{1,0:T(8,128)(2,1)S(1)}, bf16[512,256]{1,0:T(8,128)(2,1)S(1)}, u32[]{:S(2)}, u32[]{:S(2)}) collective-permute-start(bf16[512,256]{1,0:T(8,128)(2,1)S(1)} %get-tuple-element.26), channel_id=1, source_target_pairs={{0,8},{8,0},{16,24},{24,16},{1,9},{9,1},{17,25},{25,17},{2,10},{10... | collective-permute-start | bytes 786440 | tf_op jit(solution)/shard_map/ppermute | solution.py:188
  24.5 2.0 %collective-permute-start.6 = (bf16[512,256]{1,0:T(8,128)(2,1)S(1)}, bf16[512,256]{1,0:T(8,128)(2,1)S(1)}, u32[]{:S(2)}, u32[]{:S(2)}) collective-permute-start(bf16[512,256]{1,0:T(8,128)(2,1)S(1)} %get-tuple-element.22), channel_id=1, source_target_pairs={{0,16},{8,24},{16,0},{24,8},{1,17},{9,25},{17,1},{25,9},{2,18},{10... | collective-permute-start | bytes 786440 | tf_op jit(solution)/shard_map/ppermute | solution.py:184
  26.5 0.0 collective-permute-done.7.dk_in
  26.5 0.0 collective-permute-done.8.dv_in
  26.6 0.1 pieces.1
  26.7 1.5 %collective-permute-start.9 = (bf16[2,64,256]{2,1,0:T(8,128)(2,1)S(1)}, bf16[2,64,256]{2,1,0:T(8,128)(2,1)S(1)}, u32[]{:S(2)}, u32[]{:S(2)}) collective-permute-start(bf16[2,64,256]{2,1,0:T(8,128)(2,1)S(1)} %get-tuple-element.28), channel_id=1, source_target_pairs={{0,1},{1,2},{2,3},{3,4},{4,5},{5,6},{6,7},{7,0},{8,9},{9,10},{10,1... | collective-permute-start | bytes 196616 | tf_op jit(solution)/shard_map/ppermute | solution.py:184
  28.2 1.6 %collective-permute-start.10 = (bf16[2,64,256]{2,1,0:T(8,128)(2,1)S(1)}, bf16[2,64,256]{2,1,0:T(8,128)(2,1)S(1)}, u32[]{:S(2)}, u32[]{:S(2)}) collective-permute-start(bf16[2,64,256]{2,1,0:T(8,128)(2,1)S(1)} %get-tuple-element.29), channel_id=1, source_target_pairs={{0,2},{1,3},{2,4},{3,5},{4,6},{5,7},{6,0},{7,1},{8,10},{9,11},{10,... | collective-permute-start | bytes 196616 | tf_op jit(solution)/shard_map/ppermute | solution.py:184
  29.8 2.6 %collective-permute-start.11 = (bf16[2,64,256]{2,1,0:T(8,128)(2,1)S(1)}, bf16[2,64,256]{2,1,0:T(8,128)(2,1)S(1)}, u32[]{:S(2)}, u32[]{:S(2)}) collective-permute-start(bf16[2,64,256]{2,1,0:T(8,128)(2,1)S(1)} %get-tuple-element.30), channel_id=1, source_target_pairs={{0,3},{1,4},{2,5},{3,6},{4,7},{5,0},{6,1},{7,2},{8,11},{9,12},{10,... | collective-permute-start | bytes 196616 | tf_op jit(solution)/shard_map/ppermute | solution.py:184
  32.4 1.2 %collective-permute-start.12 = (bf16[2,64,256]{2,1,0:T(8,128)(2,1)S(1)}, bf16[2,64,256]{2,1,0:T(8,128)(2,1)S(1)}, u32[]{:S(2)}, u32[]{:S(2)}) collective-permute-start(bf16[2,64,256]{2,1,0:T(8,128)(2,1)S(1)} %get-tuple-element.31), channel_id=1, source_target_pairs={{0,4},{1,5},{2,6},{3,7},{4,0},{5,1},{6,2},{7,3},{8,12},{9,13},{10,... | collective-permute-start | bytes 196616 | tf_op jit(solution)/shard_map/ppermute | solution.py:184
  33.6 0.0 collective-permute-done.6
  33.6 3.0 %collective-permute-start.13 = (bf16[2,64,256]{2,1,0:T(8,128)(2,1)S(1)}, bf16[2,64,256]{2,1,0:T(8,128)(2,1)S(1)}, u32[]{:S(2)}, u32[]{:S(2)}) collective-permute-start(bf16[2,64,256]{2,1,0:T(8,128)(2,1)S(1)} %get-tuple-element.32), channel_id=1, source_target_pairs={{0,5},{1,6},{2,7},{3,0},{4,1},{5,2},{6,3},{7,4},{8,13},{9,14},{10,... | collective-permute-start | bytes 196616 | tf_op jit(solution)/shard_map/ppermute | solution.py:184
  36.6 0.0 collective-permute-done.9
  36.6 1.3 %collective-permute-start.14 = (bf16[2,64,256]{2,1,0:T(8,128)(2,1)S(1)}, bf16[2,64,256]{2,1,0:T(8,128)(2,1)S(1)}, u32[]{:S(2)}, u32[]{:S(2)}) collective-permute-start(bf16[2,64,256]{2,1,0:T(8,128)(2,1)S(1)} %get-tuple-element.33), channel_id=1, source_target_pairs={{0,6},{1,7},{2,0},{3,1},{4,2},{5,3},{6,4},{7,5},{8,14},{9,15},{10,... | collective-permute-start | bytes 196616 | tf_op jit(solution)/shard_map/ppermute | solution.py:184
  38.0 0.0 collective-permute-done.10
  38.0 1.0 %collective-permute-start.15 = (bf16[2,64,256]{2,1,0:T(8,128)(2,1)S(1)}, bf16[2,64,256]{2,1,0:T(8,128)(2,1)S(1)}, u32[]{:S(2)}, u32[]{:S(2)}) collective-permute-start(bf16[2,64,256]{2,1,0:T(8,128)(2,1)S(1)} %get-tuple-element.34), channel_id=1, source_target_pairs={{0,7},{1,0},{2,1},{3,2},{4,3},{5,4},{6,5},{7,6},{8,15},{9,8},{10,9... | collective-permute-start | bytes 196616 | tf_op jit(solution)/shard_map/ppermute | solution.py:184
  39.0 0.8 %fusion = bf16[1,512,256]{2,1,0:T(8,128)(2,1)} fusion(f32[512,256]{1,0:T(8,128)S(1)} %get-tuple-element.21, bf16[512,256]{1,0:T(8,128)(2,1)S(1)} %collective-permute-done.6), kind=kLoop, calls=%fused_computation.1 | loop fusion | flops 524288 | bytes 1048576 | tf_op jit(solution)/shard_map/broadcast_in_dim | solution.py:272
  39.8 0.0 collective-permute-done.11
  39.8 0.0 collective-permute-done.12
  39.8 2.1 %collective-permute-done.13 = bf16[2,64,256]{2,1,0:T(8,128)(2,1)S(1)} collective-permute-done((bf16[2,64,256]{2,1,0:T(8,128)(2,1)S(1)}, bf16[2,64,256]{2,1,0:T(8,128)(2,1)S(1)}, u32[]{:S(2)}, u32[]{:S(2)}) %collective-permute-start.13) | collective-permute-done | bytes 65568 | tf_op jit(solution)/shard_map/ppermute | solution.py:184
  41.9 0.5 %collective-permute-done.14 = bf16[2,64,256]{2,1,0:T(8,128)(2,1)S(1)} collective-permute-done((bf16[2,64,256]{2,1,0:T(8,128)(2,1)S(1)}, bf16[2,64,256]{2,1,0:T(8,128)(2,1)S(1)}, u32[]{:S(2)}, u32[]{:S(2)}) %collective-permute-start.14) | collective-permute-done | bytes 65568 | tf_op jit(solution)/shard_map/ppermute | solution.py:184
  42.4 0.0 collective-permute-done.15
  42.4 0.1 convert_add_fusion
  42.5 0.7 %fusion.1 = (f32[1,64,256]{2,1,0:T(8,128)}, f32[1,64,256]{2,1,0:T(8,128)}) fusion(f32[2,64,256]{2,1,0:T(8,128)S(1)} %convert_add_fusion), kind=kLoop, calls=%fused_computation.3 | loop fusion | bytes 262144 | tf_op jit(solution)/shard_map/slice | solution.py:300
Async XLA Ops:
  0.6 3.6 %collective-permute-start = (bf16[512,256]{1,0:T(8,128)(2,1)}, bf16[512,256]{1,0:T(8,128)(2,1)S(1)}, u32[]{:S(2)}, u32[]{:S(2)}) collective-permute-start(bf16[512,256]{1,0:T(8,128)(2,1)} %bitcast.12), channel_id=1, source_target_pairs={{0,8},{8,0},{16,24},{24,16},{1,9},{9,1},{17,25},{25,17},{2,10},{10... | collective-permute-start | bytes 786440 | tf_op jit(solution)/shard_map/ppermute | solution.py:188
  1.2 3.0 %collective-permute-start.1 = (bf16[512,256]{1,0:T(8,128)(2,1)}, bf16[512,256]{1,0:T(8,128)(2,1)S(1)}, u32[]{:S(2)}, u32[]{:S(2)}) collective-permute-start(bf16[512,256]{1,0:T(8,128)(2,1)} %bitcast.17), channel_id=1, source_target_pairs={{0,8},{8,0},{16,24},{24,16},{1,9},{9,1},{17,25},{25,17},{2,10},{10... | collective-permute-start | bytes 786440 | tf_op jit(solution)/shard_map/ppermute | solution.py:188
  1.3 3.0 %copy-start.8 = (s32[1,8]{1,0:T(1,128)S(1)}, s32[1,8]{1,0:T(1,128)}, u32[]{:S(2)}) copy-start(s32[1,8]{1,0:T(1,128)} %refs_0_.3) | copy-start | bytes 100
  1.3 3.0 %copy-start.9 = (s32[8]{0:T(128)S(1)}, s32[8]{0:T(128)}, u32[]{:S(2)}) copy-start(s32[8]{0:T(128)} %refs_1_.3) | copy-start | bytes 100
  1.3 10.5 %collective-permute-start.2 = (bf16[512,256]{1,0:T(8,128)(2,1)}, bf16[512,256]{1,0:T(8,128)(2,1)S(1)}, u32[]{:S(2)}, u32[]{:S(2)}) collective-permute-start(bf16[512,256]{1,0:T(8,128)(2,1)} %bitcast.6), channel_id=1, source_target_pairs={{0,16},{8,24},{16,0},{24,8},{1,17},{9,25},{17,1},{25,9},{2,18},{10... | collective-permute-start | bytes 786440 | tf_op jit(solution)/shard_map/ppermute | solution.py:184
  4.2 12.5 %collective-permute-start.3 = (bf16[512,256]{1,0:T(8,128)(2,1)}, bf16[512,256]{1,0:T(8,128)(2,1)S(1)}, u32[]{:S(2)}, u32[]{:S(2)}) collective-permute-start(bf16[512,256]{1,0:T(8,128)(2,1)} %bitcast.9), channel_id=1, source_target_pairs={{0,16},{8,24},{16,0},{24,8},{1,17},{9,25},{17,1},{25,9},{2,18},{10... | collective-permute-start | bytes 786440 | tf_op jit(solution)/shard_map/ppermute | solution.py:184
  4.3 1.0 %copy-start = (bf16[1,512,256]{2,1,0:T(8,128)(2,1)S(1)}, bf16[1,512,256]{2,1,0:T(8,128)(2,1)}, u32[]{:S(2)}) copy-start(bf16[1,512,256]{2,1,0:T(8,128)(2,1)} %param.6) | copy-start | bytes 786436
  5.2 0.9 %copy-start.2 = (bf16[1,512,256]{2,1,0:T(8,128)(2,1)S(1)}, bf16[1,512,256]{2,1,0:T(8,128)(2,1)}, u32[]{:S(2)}) copy-start(bf16[1,512,256]{2,1,0:T(8,128)(2,1)} %param.9) | copy-start | bytes 786436
  6.2 0.9 %copy-start.4 = (bf16[1,512,256]{2,1,0:T(8,128)(2,1)S(1)}, bf16[1,512,256]{2,1,0:T(8,128)(2,1)}, u32[]{:S(2)}) copy-start(bf16[1,512,256]{2,1,0:T(8,128)(2,1)} %param.7) | copy-start | bytes 786436
  7.1 0.9 %copy-start.6 = (bf16[1,512,256]{2,1,0:T(8,128)(2,1)S(1)}, bf16[1,512,256]{2,1,0:T(8,128)(2,1)}, u32[]{:S(2)}) copy-start(bf16[1,512,256]{2,1,0:T(8,128)(2,1)} %param.8) | copy-start | bytes 786436
  8.1 8.6 %copy-start.5 = (bf16[1,512,256]{2,1,0:T(8,128)(2,1)S(1)}, bf16[1,512,256]{2,1,0:T(8,128)(2,1)}, u32[]{:S(2)}) copy-start(bf16[1,512,256]{2,1,0:T(8,128)(2,1)} %param.7) | copy-start | bytes 786436
  8.1 8.6 %copy-start.7 = (bf16[1,512,256]{2,1,0:T(8,128)(2,1)S(1)}, bf16[1,512,256]{2,1,0:T(8,128)(2,1)}, u32[]{:S(2)}) copy-start(bf16[1,512,256]{2,1,0:T(8,128)(2,1)} %param.8) | copy-start | bytes 786436
  9.8 10.1 %collective-permute-start.5 = (f32[3,512]{1,0:T(4,128)S(1)}, f32[3,512]{1,0:T(4,128)S(1)}, u32[]{:S(2)}, u32[]{:S(2)}) collective-permute-start(f32[3,512]{1,0:T(4,128)S(1)} %stats0.1.refs_8_), channel_id=1, source_target_pairs={{0,16},{8,24},{16,0},{24,8},{1,17},{9,25},{17,1},{25,9},{2,18},{10... | collective-permute-start | bytes 18440 | tf_op jit(solution)/shard_map/ppermute | solution.py:184
  17.3 4.1 %copy-start.1 = (bf16[1,512,256]{2,1,0:T(8,128)(2,1)S(1)}, bf16[1,512,256]{2,1,0:T(8,128)(2,1)}, u32[]{:S(2)}) copy-start(bf16[1,512,256]{2,1,0:T(8,128)(2,1)} %param.6) | copy-start | bytes 786436
  17.3 4.1 %copy-start.3 = (bf16[1,512,256]{2,1,0:T(8,128)(2,1)S(1)}, bf16[1,512,256]{2,1,0:T(8,128)(2,1)}, u32[]{:S(2)}) copy-start(bf16[1,512,256]{2,1,0:T(8,128)(2,1)} %param.9) | copy-start | bytes 786436
  17.4 4.1 %collective-permute-start.4 = (f32[3,512]{1,0:T(4,128)S(1)}, f32[3,512]{1,0:T(4,128)S(1)}, u32[]{:S(2)}, u32[]{:S(2)}) collective-permute-start(f32[3,512]{1,0:T(4,128)S(1)} %stats1.1.refs_8_), channel_id=1, source_target_pairs={{0,16},{8,24},{16,0},{24,8},{1,17},{9,25},{17,1},{25,9},{2,18},{10... | collective-permute-start | bytes 18440 | tf_op jit(solution)/shard_map/ppermute | solution.py:184
  23.9 2.6 %collective-permute-start.7 = (bf16[512,256]{1,0:T(8,128)(2,1)S(1)}, bf16[512,256]{1,0:T(8,128)(2,1)S(1)}, u32[]{:S(2)}, u32[]{:S(2)}) collective-permute-start(bf16[512,256]{1,0:T(8,128)(2,1)S(1)} %get-tuple-element.25), channel_id=1, source_target_pairs={{0,8},{8,0},{16,24},{24,16},{1,9},{9,1},{17,25},{25,17},{2,10},{10... | collective-permute-start | bytes 786440 | tf_op jit(solution)/shard_map/ppermute | solution.py:188
  24.0 2.5 %collective-permute-start.8 = (bf16[512,256]{1,0:T(8,128)(2,1)S(1)}, bf16[512,256]{1,0:T(8,128)(2,1)S(1)}, u32[]{:S(2)}, u32[]{:S(2)}) collective-permute-start(bf16[512,256]{1,0:T(8,128)(2,1)S(1)} %get-tuple-element.26), channel_id=1, source_target_pairs={{0,8},{8,0},{16,24},{24,16},{1,9},{9,1},{17,25},{25,17},{2,10},{10... | collective-permute-start | bytes 786440 | tf_op jit(solution)/shard_map/ppermute | solution.py:188
  24.5 9.1 %collective-permute-start.6 = (bf16[512,256]{1,0:T(8,128)(2,1)S(1)}, bf16[512,256]{1,0:T(8,128)(2,1)S(1)}, u32[]{:S(2)}, u32[]{:S(2)}) collective-permute-start(bf16[512,256]{1,0:T(8,128)(2,1)S(1)} %get-tuple-element.22), channel_id=1, source_target_pairs={{0,16},{8,24},{16,0},{24,8},{1,17},{9,25},{17,1},{25,9},{2,18},{10... | collective-permute-start | bytes 786440 | tf_op jit(solution)/shard_map/ppermute | solution.py:184
  26.7 9.9 %collective-permute-start.9 = (bf16[2,64,256]{2,1,0:T(8,128)(2,1)S(1)}, bf16[2,64,256]{2,1,0:T(8,128)(2,1)S(1)}, u32[]{:S(2)}, u32[]{:S(2)}) collective-permute-start(bf16[2,64,256]{2,1,0:T(8,128)(2,1)S(1)} %get-tuple-element.28), channel_id=1, source_target_pairs={{0,1},{1,2},{2,3},{3,4},{4,5},{5,6},{6,7},{7,0},{8,9},{9,10},{10,1... | collective-permute-start | bytes 196616 | tf_op jit(solution)/shard_map/ppermute | solution.py:184
  28.2 9.7 %collective-permute-start.10 = (bf16[2,64,256]{2,1,0:T(8,128)(2,1)S(1)}, bf16[2,64,256]{2,1,0:T(8,128)(2,1)S(1)}, u32[]{:S(2)}, u32[]{:S(2)}) collective-permute-start(bf16[2,64,256]{2,1,0:T(8,128)(2,1)S(1)} %get-tuple-element.29), channel_id=1, source_target_pairs={{0,2},{1,3},{2,4},{3,5},{4,6},{5,7},{6,0},{7,1},{8,10},{9,11},{10,... | collective-permute-start | bytes 196616 | tf_op jit(solution)/shard_map/ppermute | solution.py:184
  29.8 10.0 %collective-permute-start.11 = (bf16[2,64,256]{2,1,0:T(8,128)(2,1)S(1)}, bf16[2,64,256]{2,1,0:T(8,128)(2,1)S(1)}, u32[]{:S(2)}, u32[]{:S(2)}) collective-permute-start(bf16[2,64,256]{2,1,0:T(8,128)(2,1)S(1)} %get-tuple-element.30), channel_id=1, source_target_pairs={{0,3},{1,4},{2,5},{3,6},{4,7},{5,0},{6,1},{7,2},{8,11},{9,12},{10,... | collective-permute-start | bytes 196616 | tf_op jit(solution)/shard_map/ppermute | solution.py:184
  32.4 7.4 %collective-permute-start.12 = (bf16[2,64,256]{2,1,0:T(8,128)(2,1)S(1)}, bf16[2,64,256]{2,1,0:T(8,128)(2,1)S(1)}, u32[]{:S(2)}, u32[]{:S(2)}) collective-permute-start(bf16[2,64,256]{2,1,0:T(8,128)(2,1)S(1)} %get-tuple-element.31), channel_id=1, source_target_pairs={{0,4},{1,5},{2,6},{3,7},{4,0},{5,1},{6,2},{7,3},{8,12},{9,13},{10,... | collective-permute-start | bytes 196616 | tf_op jit(solution)/shard_map/ppermute | solution.py:184
  33.6 8.3 %collective-permute-start.13 = (bf16[2,64,256]{2,1,0:T(8,128)(2,1)S(1)}, bf16[2,64,256]{2,1,0:T(8,128)(2,1)S(1)}, u32[]{:S(2)}, u32[]{:S(2)}) collective-permute-start(bf16[2,64,256]{2,1,0:T(8,128)(2,1)S(1)} %get-tuple-element.32), channel_id=1, source_target_pairs={{0,5},{1,6},{2,7},{3,0},{4,1},{5,2},{6,3},{7,4},{8,13},{9,14},{10,... | collective-permute-start | bytes 196616 | tf_op jit(solution)/shard_map/ppermute | solution.py:184
  36.6 5.8 %collective-permute-start.14 = (bf16[2,64,256]{2,1,0:T(8,128)(2,1)S(1)}, bf16[2,64,256]{2,1,0:T(8,128)(2,1)S(1)}, u32[]{:S(2)}, u32[]{:S(2)}) collective-permute-start(bf16[2,64,256]{2,1,0:T(8,128)(2,1)S(1)} %get-tuple-element.33), channel_id=1, source_target_pairs={{0,6},{1,7},{2,0},{3,1},{4,2},{5,3},{6,4},{7,5},{8,14},{9,15},{10,... | collective-permute-start | bytes 196616 | tf_op jit(solution)/shard_map/ppermute | solution.py:184
  38.0 4.5 %collective-permute-start.15 = (bf16[2,64,256]{2,1,0:T(8,128)(2,1)S(1)}, bf16[2,64,256]{2,1,0:T(8,128)(2,1)S(1)}, u32[]{:S(2)}, u32[]{:S(2)}) collective-permute-start(bf16[2,64,256]{2,1,0:T(8,128)(2,1)S(1)} %get-tuple-element.34), channel_id=1, source_target_pairs={{0,7},{1,0},{2,1},{3,2},{4,3},{5,4},{6,5},{7,6},{8,15},{9,8},{10,9... | collective-permute-start | bytes 196616 | tf_op jit(solution)/shard_map/ppermute | solution.py:184

commit v3 on v0

v3 whole, which is shorter than its diff:
```python
import functools
import math

import jax
import jax.numpy as jnp
from jax import lax
from jax.experimental import pallas as pl
from jax.experimental.pallas import tpu as pltpu
from jax.sharding import PartitionSpec as P


HEAD_COUNT = 8
MASKED = -1e30
VMEM_LIMIT = 14 * 1024 * 1024
CORES = 2


def contract(left, right, left_dim, right_dim):
    return lax.dot_general(
        left, right, (((left_dim,), (right_dim,)), ((), ())), preferred_element_type=jnp.float32
    )


def place_body(local, docs, fold, *refs):
    for source, target in zip(refs[:4], refs[4:8]):
        target[...] = source[...]
    outs = refs[8:]
    seq_total = lax.axis_size("seq")
    per_shard = fold.shape[0] // seq_total
    block = local // per_shard
    own = lax.axis_index("seq")
    row = lax.axis_index("head") // HEAD_COUNT
    starts = [jnp.int32(0)]
    for d in range(docs.shape[1] - 1):
        starts.append(starts[-1] + docs[row, d])
    key_bases = [
        fold[shard * per_shard + j] * block for shard in (own, own ^ 1) for j in range(per_shard)
    ]
    for offset in range(len(outs) // 2):
        info, word = outs[2 * offset : 2 * offset + 2]
        shard = lax.rem(own + offset * CORES, seq_total)
        bits = jnp.int32(0)
        for i in range(per_shard):
            base = fold[shard * per_shard + i] * block
            position = base + lax.broadcasted_iota(jnp.int32, (1, block), 1)
            start = jnp.zeros((1, block), jnp.int32)
            first = jnp.int32(0)
            for d in starts[1:]:
                start = jnp.where(position >= d, d, start)
                first = jnp.where(base >= d, d, first)
            for j, key_base in enumerate(key_bases):
                tile = i * len(key_bases) + j
                info[2 * tile : 2 * tile + 1, :] = start - key_base
                info[2 * tile + 1 : 2 * tile + 2, :] = position - key_base
                active = (key_base <= base) & (key_base + block > first)
                bits = bits | jnp.where(active, 1 << tile, 0)
        word[...] = jnp.full(word.shape, bits, jnp.int32)


def tile_bit(bits, tile):
    return ((bits >> tile) & 1) == 1


def stats_body(factor, info, word, query, grad, *refs):
    keys, values = refs[0:2], refs[2:4]
    out, scores_out, prob_out = refs[4:]
    local = query.shape[0]
    block = info.shape[1]
    per_shard = local // block
    bits = jnp.max(word[...])
    key_index = lax.broadcasted_iota(jnp.int32, (block, block), 0)
    for i in range(per_shard):
        rows = pl.ds(i * block, block)
        out[0:1, rows] = jnp.full((1, block), MASKED, jnp.float32)
        out[1:3, rows] = jnp.zeros((2, block), jnp.float32)
        for j in range(CORES * per_shard):
            tile = i * CORES * per_shard + j
            side, cols = j // per_shard, pl.ds(j % per_shard * block, block)
            held = pl.ds(j * block, block)

            @pl.when(tile_bit(bits, tile))
            def _():
                allowed = (key_index >= info[2 * tile : 2 * tile + 1, :]) & (
                    key_index <= info[2 * tile + 1 : 2 * tile + 2, :]
                )
                scores = contract(keys[side][cols, :], query[rows, :], 1, 1) * factor
                scores = jnp.where(allowed, scores, MASKED)
                prob = contract(values[side][cols, :], grad[rows, :], 1, 1)
                scores_out[held, rows] = scores
                prob_out[held, rows] = prob
                old_max = out[0:1, rows]
                new_max = jnp.maximum(old_max, jnp.max(scores, axis=0, keepdims=True))
                keep = jnp.exp2(old_max - new_max)
                weights = jnp.exp2(scores - new_max)
                out[0:1, rows] = new_max
                out[1:2, rows] = out[1:2, rows] * keep + jnp.sum(weights, axis=0, keepdims=True)
                out[2:3, rows] = out[2:3, rows] * keep + jnp.sum(
                    weights * prob, axis=0, keepdims=True
                )


def grads_body(parts, first, last, word, scores, probs, query, grad, *refs):
    keys = refs[0:2]
    stats = refs[2 : 2 + parts]
    rest = list(refs[2 + parts :])
    prior = None if first else (rest.pop(0), rest.pop(0))
    dq = rest.pop(0)
    outs = [rest.pop(0) for _ in range(4 if last else 2)]
    acc_key, acc_value, acc_query = rest
    local = query.shape[0]
    block = acc_query.shape[0]
    per_shard = local // block
    tiles = CORES * per_shard
    bits = jnp.max(word[...])
    top = stats[0][0:1, :]
    for part in stats[1:]:
        top = jnp.maximum(top, part[0:1, :])
    total = jnp.zeros_like(top)
    dots = jnp.zeros_like(top)
    for part in stats:
        keep = jnp.exp2(part[0:1, :] - top)
        total = total + part[1:2, :] * keep
        dots = dots + part[2:3, :] * keep
    norm = top + jnp.log2(total)
    dots = dots / total

    def settle(active, target, source, term):
        ref, at = target
        if active:
            value = term()
            if source is not None:
                value = value + source[0][source[1], :]
            ref[at, :] = value.astype(ref.dtype)
        elif source is None:
            ref[at, :] = jnp.zeros((block, ref.shape[1]), ref.dtype)
        elif source[0] is not ref:
            ref[at, :] = source[0][source[1], :].astype(ref.dtype)

    for i in range(per_shard):
        rows = pl.ds(i * block, block)
        norm_i = norm[:, i * block : (i + 1) * block]
        dots_i = dots[:, i * block : (i + 1) * block]
        for j in range(tiles):
            side, cols = j // per_shard, pl.ds(j % per_shard * block, block)
            held = pl.ds(j * block, block)
            query_source = None if j == 0 else (acc_query, pl.ds(0, block))
            query_target = (dq, rows) if j == tiles - 1 else (acc_query, pl.ds(0, block))
            sources = []
            targets = []
            for n, acc in enumerate((acc_key, acc_value)):
                if i > 0:
                    sources.append((acc, held))
                else:
                    sources.append(None if first else (prior[n], held))
                if i < per_shard - 1:
                    targets.append((acc, held))
                elif last:
                    targets.append((outs[n + 2 * side], cols))
                else:
                    targets.append((outs[n], held))
            bit = tile_bit(bits, i * tiles + j)

            @pl.when(bit)
            def _():
                g, q = grad[rows, :], query[rows, :]
                weights = jnp.exp2(scores[held, rows] - norm_i)
                slope = (weights * (probs[held, rows] - dots_i)).astype(jnp.bfloat16)
                settle(
                    True,
                    targets[1],
                    sources[1],
                    lambda: contract(weights.astype(jnp.bfloat16), g, 1, 0),
                )
                settle(True, targets[0], sources[0], lambda: contract(slope, q, 1, 0))
                settle(
                    True,
                    query_target,
                    query_source,
                    lambda: contract(slope, keys[side][cols, :], 0, 0),
                )

            @pl.when(jnp.logical_not(bit))
            def _():
                settle(False, targets[1], sources[1], None)
                settle(False, targets[0], sources[0], None)
                settle(False, query_target, query_source, None)


def split_body(scaling, order, dk, dv, dk_in, dv_in, *outs):
    head = lax.axis_index("head")
    piece = outs[0].shape[1]
    for step, out in zip([0] + order, outs):
        rows = pl.ds(pl.multiple_of(lax.rem(head + step, lax.axis_size("head")) * piece, piece), piece)
        key_sum = (dk[rows, :] + dk_in[rows, :].astype(jnp.float32)) * scaling
        value_sum = dv[rows, :] + dv_in[rows, :].astype(jnp.float32)
        out[0] = key_sum.astype(out.dtype)
        out[1] = value_sum.astype(out.dtype)


def exchange_order(heads):
    return list(range(1, heads))


def by_row(row_count, steps, terms):
    head = lax.axis_index("head")
    rows = []
    for r in range(row_count):
        total = None
        for step, term in zip(steps, terms):
            term = term.astype(jnp.float32)
            if row_count > 1:
                term = jnp.where(lax.rem(head - step + lax.axis_size("head"), lax.axis_size("head")) // HEAD_COUNT == r, term, 0.0)
            total = term if total is None else total + term
        rows.append(total)
    return rows


SMEM = pl.BlockSpec(memory_space=pltpu.SMEM)
VMEM = pl.BlockSpec(memory_space=pltpu.VMEM)


def shift(x, axis, amount):
    size = lax.axis_size(axis)
    return lax.ppermute(x, axis, [(i, (i - amount) % size) for i in range(size)])


def swap_cores(x):
    return lax.ppermute(x, "seq", [(i, i ^ 1) for i in range(lax.axis_size("seq"))])


def kernel(body, operands, outs, flops, scratch=()):
    return pl.pallas_call(
        body,
        out_shape=outs,
        in_specs=[SMEM if x.dtype == jnp.int32 and x.ndim < 2 else VMEM for x in operands],
        out_specs=[VMEM] * len(outs),
        scratch_shapes=list(scratch),
        compiler_params=pltpu.CompilerParams(vmem_limit_bytes=VMEM_LIMIT),
        cost_estimate=pl.CostEstimate(
            flops=int(flops), bytes_accessed=int(flops) // 256, transcendentals=0
        ),
    )(*operands)


def gradients(queries, keys, values, d_out, doc_lengths, fold_order):
    local, width = queries.shape[1:]
    chips = lax.axis_size("seq") // CORES
    heads = lax.axis_size("head")
    row_count = keys.shape[0]
    piece = local // heads
    block = local // (fold_order.shape[0] // lax.axis_size("seq"))
    tiles = (local // block) * (CORES * local // block)
    scaling = width ** (-0.5)
    factor = scaling * math.log2(math.e)
    row_index = lax.axis_index("head") // HEAD_COUNT
    full = jnp.float32
    low = jnp.bfloat16
    shape = jax.ShapeDtypeStruct

    sets = [(queries[0], d_out[0])]
    for offset in range(1, chips):
        sets.append(
            (shift(queries[0], "seq", offset * CORES), shift(d_out[0], "seq", offset * CORES))
        )
    if row_count == 1:
        key_own, value_own = keys[0], values[0]
    else:
        key_own = lax.dynamic_index_in_dim(keys, row_index, 0, keepdims=False)
        value_own = lax.dynamic_index_in_dim(values, row_index, 0, keepdims=False)
    key_sib, value_sib = swap_cores(key_own), swap_cores(value_own)
    own_arrays = (*sets[0], key_own, value_own)
    places = pl.pallas_call(
        functools.partial(place_body, local),
        out_shape=[shape((local, width), low)] * 4
        + [shape((2 * tiles, block), jnp.int32), shape((8, 128), jnp.int32)] * chips,
        in_specs=[SMEM] * 2 + [VMEM] * 4,
        out_specs=[VMEM] * (4 + 2 * chips),
        name="place",
        compiler_params=pltpu.CompilerParams(vmem_limit_bytes=VMEM_LIMIT),
        cost_estimate=pl.CostEstimate(flops=1 << 20, bytes_accessed=1 << 14, transcendentals=0),
    )(doc_lengths, fold_order, *own_arrays)
    sets[0] = tuple(places[:2])
    key_own, value_own = places[2:4]
    places = places[4:]

    work = 4 * local * CORES * local * width
    stats, held = [], []
    for offset in range(chips):
        info, word = places[2 * offset : 2 * offset + 2]
        pairs = shape((CORES * local, local), full)
        part, scores, probs = kernel(
            functools.partial(stats_body, factor),
            (info, word, *sets[offset], key_own, key_sib, value_own, value_sib),
            [shape((3, local), full), pairs, pairs],
            work,
        )
        stats.append(part)
        held.append((word, scores, probs))
    far = {
        (step, offset): shift(stats[(offset - step) % chips], "seq", step * CORES)
        for step in range(1, chips)
        for offset in range(chips)
    }
    acc = ()
    partial_queries = [None] * chips
    for n, offset in enumerate(list(range(1, chips)) + [0]):
        first, last = n == 0, n == chips - 1
        parts = [stats[offset]] + [far[step, offset] for step in range(1, chips)]
        mine, sent = shape((local, width), full), shape((local, width), low)
        wide = shape((CORES * local, width), full)
        results = kernel(
            functools.partial(grads_body, chips, first, last),
            (*held[offset], *sets[offset], key_own, key_sib, *parts, *acc),
            [mine if offset == 0 else sent] + ([mine, mine, sent, sent] if last else [wide, wide]),
            1.5 * work,
            [pltpu.VMEM((CORES * local, width), full)] * 2 + [pltpu.VMEM((block, width), full)],
        )
        partial_queries[offset] = results[0]
        acc = results[1:]
    dk, dv, dk_out, dv_out = acc
    dk_in, dv_in = swap_cores(dk_out), swap_cores(dv_out)
    grad_query = partial_queries[0]
    for offset in range(1, chips):
        grad_query = grad_query + shift(
            partial_queries[offset], "seq", -offset * CORES
        ).astype(full)
    grad_queries = (grad_query * scaling).astype(low)[None]

    order = exchange_order(heads)
    moved = kernel(
        functools.partial(split_body, scaling, order),
        (dk, dv, dk_in, dv_in),
        [shape((2, piece, width), full)] + [shape((2, piece, width), low)] * (heads - 1),
        4 * local * width,
    )
    terms = [moved[0]]
    for step, x in zip(order, moved[1:]):
        terms.append(shift(x, "head", -step))
    rows = by_row(row_count, [0] + order, terms)
    grad_keys = jnp.stack([total[0] for total in rows])
    grad_values = jnp.stack([total[1] for total in rows])
    return grad_queries, grad_keys, grad_values


def solution(mesh):
    in_specs = (
        P("head", "seq", None),
        P(None, "seq", None),
        P(None, "seq", None),
        P("head", "seq", None),
        P(),
        P(),
    )
    out_specs = (
        P("head", "seq", None),
        P(None, ("seq", "head"), None),
        P(None, ("seq", "head"), None),
    )
    return jax.shard_map(
        gradients, mesh=mesh, in_specs=in_specs, out_specs=out_specs, check_vma=False
    )
```

time: 124 us -> 42 us (0.34)
  waiting for transfers between devices: 73.8 us -> 6.99 us
  matrix products: 16.5 us -> 0 us
  between operations: 13.9 us -> 0.73 us
  starting transfers between devices: 11.2 us -> 22.1 us
  other arithmetic: 6.24 us -> 0.83 us
  Pallas kernels: 0 us -> 5.33 us
  local copies, waits for them, and re-layouts: 1.69 us -> 5.77 us
    reduce_scatter x2 -> x0, waiting for transfers between devices: 39.6 us -> none  [the longest x1 21.7 us: per_device(): lax.psum_scatter(full_keys.astype(jnp.bfloat16), 'seq', scatter_dimension...]
    all_gather x2 -> x0, waiting for transfers between devices: 27.7 us -> none  [the longest x1 17.1 us: per_device(): key_part = lax.all_gather(key_row, 'seq', axis=0, tiled=True)]
    ppermute x0 -> x16, starting transfers between devices: none -> 22.1 us  [the longest x12 20.9 us: shift(): lax.ppermute(x, axis, [(i, (i - amount) % size) for i in range(size)])]
    dot_general x6 -> x0, matrix products: 16.5 us -> none  [the longest x2 4.69 us: contract_first(): lax.dot_general(left, right, (((0,), (0,)), ((), ())), preferred_element_...]
    all_to_all x2 -> x0, starting transfers between devices: 11 us -> none  [the longest x1 5.51 us: owner_blocks(): lax.all_to_all(key_part.astype(jnp.bfloat16), 'head', split_axis=0, conca...]
    ppermute x0 -> x16, waiting for transfers between devices: none -> 6.99 us  [the longest x12 6.98 us: shift(): lax.ppermute(x, axis, [(i, (i - amount) % size) for i in range(size)])]
    pallas_call x0 -> x6, Pallas kernels: none -> 5.33 us  [the longest x5 4.69 us: kernel(): pl.pallas_call(body, out_shape=outs, in_specs=[SMEM if x.dtype == jnp.int...]
    all_to_all x2 -> x0, waiting for transfers between devices: 5.07 us -> none  [the longest x1 5.07 us: owner_blocks(): lax.all_to_all(key_part.astype(jnp.bfloat16), 'head', split_axis=0, conca...]
  transfers between devices with their start and end apart: 6 -> 16, of which waited for: 5 -> 4; matrix products, arithmetic and copies ran while one was open for 18% -> 2% of each run, Pallas kernels for 0% -> 9%
where the time goes in v3:
time: 42 us; the launch traced here: 41.8 us
  starting transfers between devices  22.1 us (53%)
  waiting for transfers between devices  6.99 us (17%)
  local copies, waits for them, and re-layouts  5.77 us (14%)
  Pallas kernels  5.33 us (13%)
  other arithmetic  0.83 us (2%)
  between operations  0.73 us (2%)
    ppermute x12, starting transfers between devices, shift(): lax.ppermute(x, axis, [(i, (i - amount) % size) for i in range(size)])  20.9 us
    ppermute x12, waiting for transfers between devices, shift(): lax.ppermute(x, axis, [(i, (i - amount) % size) for i in range(size)])  6.98 us
    unnamed x12, local copies, waits for them, and re-layouts  5.11 us
    pallas_call x5, Pallas kernels, kernel(): pl.pallas_call(body, out_shape=outs, in_specs=[SMEM if x.dtype == jnp.int...  4.69 us
    ppermute x4, starting transfers between devices, swap_cores(): lax.ppermute(x, 'seq', [(i, i ^ 1) for i in range(lax.axis_size('seq'))])  1.2 us
  transfers between devices with their start and end apart: 16, of which 4 were waited for; matrix products, arithmetic and copies ran while one was open for 2% of the time, Pallas kernels for 9%

profile of v3, /device:TPU:0, one launch (start us, length us, event | category | flops | bytes accessed | tf_op | source)
XLA Modules:
  0.0 41.8 jit_solution(10844073666400347905)
XLA Ops:
  0.6 0.6 %collective-permute-start = (bf16[512,256]{1,0:T(8,128)(2,1)}, bf16[512,256]{1,0:T(8,128)(2,1)S(1)}, u32[]{:S(2)}, u32[]{:S(2)}) collective-permute-start(bf16[512,256]{1,0:T(8,128)(2,1)} %bitcast.6), channel_id=1, source_target_pairs={{0,8},{8,0},{16,24},{24,16},{1,9},{9,1},{17,25},{25,17},{2,10},{10... | collective-permute-start | bytes 786440 | tf_op jit(solution)/shard_map/ppermute | solution.py:228
  1.2 0.1 collective-permute-start.1
  1.3 2.9 %collective-permute-start.2 = (bf16[512,256]{1,0:T(8,128)(2,1)}, bf16[512,256]{1,0:T(8,128)(2,1)S(1)}, u32[]{:S(2)}, u32[]{:S(2)}) collective-permute-start(bf16[512,256]{1,0:T(8,128)(2,1)} %bitcast.10), channel_id=1, source_target_pairs={{0,16},{8,24},{16,0},{24,8},{1,17},{9,25},{17,1},{25,9},{2,18},{10... | collective-permute-start | bytes 786440 | tf_op jit(solution)/shard_map/ppermute | solution.py:224
  4.2 0.0 collective-permute-start.3
  4.2 0.0 copy-start
  4.2 0.9 %copy-done = bf16[1,512,256]{2,1,0:T(8,128)(2,1)S(1)} copy-done((bf16[1,512,256]{2,1,0:T(8,128)(2,1)S(1)}, bf16[1,512,256]{2,1,0:T(8,128)(2,1)}, u32[]{:S(2)}) %copy-start) | copy-done | bytes 262168
  5.2 0.0 copy-start.1
  5.2 0.9 %copy-done.1 = bf16[1,512,256]{2,1,0:T(8,128)(2,1)S(1)} copy-done((bf16[1,512,256]{2,1,0:T(8,128)(2,1)S(1)}, bf16[1,512,256]{2,1,0:T(8,128)(2,1)}, u32[]{:S(2)}) %copy-start.1) | copy-done | bytes 262168
  6.1 0.0 copy-start.2
  6.1 0.9 %copy-done.2 = bf16[1,512,256]{2,1,0:T(8,128)(2,1)S(1)} copy-done((bf16[1,512,256]{2,1,0:T(8,128)(2,1)S(1)}, bf16[1,512,256]{2,1,0:T(8,128)(2,1)}, u32[]{:S(2)}) %copy-start.2) | copy-done | bytes 262168
  7.1 0.0 copy-start.3
  7.1 0.9 %copy-done.3 = bf16[1,512,256]{2,1,0:T(8,128)(2,1)S(1)} copy-done((bf16[1,512,256]{2,1,0:T(8,128)(2,1)S(1)}, bf16[1,512,256]{2,1,0:T(8,128)(2,1)}, u32[]{:S(2)}) %copy-start.3) | copy-done | bytes 262168
  8.0 0.0 copy-start.4
  8.0 0.7 %copy-done.4 = s32[1,8]{1,0:T(1,128)S(1)} copy-done((s32[1,8]{1,0:T(1,128)S(1)}, s32[1,8]{1,0:T(1,128)}, u32[]{:S(2)}) %copy-start.4) | copy-done | bytes 56
  8.7 0.0 copy-start.5
  8.7 0.7 %copy-done.5 = s32[8]{0:T(128)S(1)} copy-done((s32[8]{0:T(128)S(1)}, s32[8]{0:T(128)}, u32[]{:S(2)}) %copy-start.5) | copy-done | bytes 56
  9.3 0.6 %place.1 = (bf16[512,256]{1,0:T(8,128)(2,1)S(1)}, bf16[512,256]{1,0:T(8,128)(2,1)S(1)}, bf16[512,256]{1,0:T(8,128)(2,1)S(1)}, bf16[512,256]{1,0:T(8,128)(2,1)S(1...) custom-call(s32[1,8]{1,0:T(1,128)S(1)} %copy-done.4, ...), custom_call_target="tpu_custom_call" | custom-call | flops 1048576 | bytes 16384 | tf_op jit(solution)/shard_map/place/pallas_call | solution.py:272
  10.0 0.0 collective-permute-done.refs_1_
  10.0 0.0 collective-permute-done.1.refs_3_
  10.0 1.6 %shard_map.85 = (f32[3,512]{1,0:T(4,128)S(1)}, f32[1024,512]{1,0:T(8,128)S(1)}, f32[1024,512]{1,0:T(8,128)S(1)}) custom-call(s32[16,256]{1,0:T(8,128)S(1)} %get-tuple-element.34.info, s32[8,128]{1,0:T(8,128)S(1)} %get-tuple-element.33.word, bf16[512,256]{1,0:T(8,128)(2,1)S(1)} %get-tuple-element.35.query, bf16[512,256]{1,0:T(8,128)(2,1)S(1)} %get-tuple-element.36.grad, ...), custom_call_target="tpu_custom_call" | custom-call | flops 536870912 | bytes 2097152 | tf_op jit(solution)/shard_map/pallas_call | solution.py:232
  11.6 1.7 %collective-permute-start.5 = (f32[3,512]{1,0:T(4,128)S(1)}, f32[3,512]{1,0:T(4,128)S(1)}, u32[]{:S(2)}, u32[]{:S(2)}) collective-permute-start(f32[3,512]{1,0:T(4,128)S(1)} %get-tuple-element.41.refs_2_), channel_id=1, source_target_pairs={{0,16},{8,24},{16,0},{24,8},{1,17},{9,25},{17,1},{25,9},{2,18},{10... | collective-permute-start | bytes 18440 | tf_op jit(solution)/shard_map/ppermute | solution.py:224
  13.3 0.0 collective-permute-done.2.query
  13.4 3.3 %collective-permute-done.3.grad = bf16[512,256]{1,0:T(8,128)(2,1)S(1)} collective-permute-done((bf16[512,256]{1,0:T(8,128)(2,1)}, bf16[512,256]{1,0:T(8,128)(2,1)S(1)}, u32[]{:S(2)}, u32[]{:S(2)}) %collective-permute-start.3) | collective-permute-done | bytes 262176 | tf_op jit(solution)/shard_map/ppermute | solution.py:224
  16.7 0.6 %shard_map.86 = (f32[3,512]{1,0:T(4,128)S(1)}, f32[1024,512]{1,0:T(8,128)S(1)}, f32[1024,512]{1,0:T(8,128)S(1)}) custom-call(s32[16,256]{1,0:T(8,128)S(1)} %get-tuple-element.42.info, s32[8,128]{1,0:T(8,128)S(1)} %get-tuple-element.43.word, bf16[512,256]{1,0:T(8,128)(2,1)S(1)} %collective-permute-done.2.query, ...), custom_call_target="tpu_custom_call" | custom-call | flops 536870912 | bytes 2097152 | tf_op jit(solution)/shard_map/pallas_call | solution.py:232
  17.3 2.1 %collective-permute-start.4 = (f32[3,512]{1,0:T(4,128)S(1)}, f32[3,512]{1,0:T(4,128)S(1)}, u32[]{:S(2)}, u32[]{:S(2)}) collective-permute-start(f32[3,512]{1,0:T(4,128)S(1)} %get-tuple-element.44.refs_2_), channel_id=1, source_target_pairs={{0,16},{8,24},{16,0},{24,8},{1,17},{9,25},{17,1},{25,9},{2,18},{10... | collective-permute-start | bytes 18440 | tf_op jit(solution)/shard_map/ppermute | solution.py:224
  19.4 0.0 collective-permute-done.5.refs_3_
  19.4 0.8 %shard_map.87 = (bf16[512,256]{1,0:T(8,128)(2,1)S(1)}, f32[1024,256]{1,0:T(8,128)S(1)}, f32[1024,256]{1,0:T(8,128)S(1)}) custom-call(s32[8,128]{1,0:T(8,128)S(1)} %get-tuple-element.43.word, f32[1024,512]{1,0:T(8,128)S(1)} %get-tuple-element.45.scores, f32[1024,512]{1,0:T(8,128)S(1)} %get-tuple-element.46.probs, ...), custom_call_target="tpu_custom_call" | custom-call | flops 805306368 | bytes 3145728 | tf_op jit(solution)/shard_map/pallas_call | solution.py:232
  20.2 0.8 %collective-permute-done.4.refs_3_ = f32[3,512]{1,0:T(4,128)S(1)} collective-permute-done((f32[3,512]{1,0:T(4,128)S(1)}, f32[3,512]{1,0:T(4,128)S(1)}, u32[]{:S(2)}, u32[]{:S(2)}) %collective-permute-start.4) | collective-permute-done | bytes 6176 | tf_op jit(solution)/shard_map/ppermute | solution.py:224
  21.0 1.6 %shard_map.88 = (f32[512,256]{1,0:T(8,128)S(1)}, f32[512,256]{1,0:T(8,128)S(1)}, f32[512,256]{1,0:T(8,128)S(1)}, bf16[512,256]{1,0:T(8,128)(2,1)S(1)}, bf16[512,256]{1,0:T(8,128)(2,1)S(1)}) custom-call(s32[8,128]{1,0:T(8,128)S(1)} %get-tuple-element.33.word, f32[1024,512]{1,0:T(8,128)S(1)} %get-tuple-element.39.scores, ...), custom_call_target="tpu_custom_call" | custom-call | flops 805306368 | bytes 3145728 | tf_op jit(solution)/shard_map/pallas_call | solution.py:232
  22.6 0.1 collective-permute-start.7
  22.7 0.5 %collective-permute-start.8 = (bf16[512,256]{1,0:T(8,128)(2,1)S(1)}, bf16[512,256]{1,0:T(8,128)(2,1)S(1)}, u32[]{:S(2)}, u32[]{:S(2)}) collective-permute-start(bf16[512,256]{1,0:T(8,128)(2,1)S(1)} %get-tuple-element.54), channel_id=1, source_target_pairs={{0,8},{8,0},{16,24},{24,16},{1,9},{9,1},{17,25},{25,17},{2,10},{10... | collective-permute-start | bytes 786440 | tf_op jit(solution)/shard_map/ppermute | solution.py:228
  23.2 1.8 %collective-permute-start.6 = (bf16[512,256]{1,0:T(8,128)(2,1)S(1)}, bf16[512,256]{1,0:T(8,128)(2,1)S(1)}, u32[]{:S(2)}, u32[]{:S(2)}) collective-permute-start(bf16[512,256]{1,0:T(8,128)(2,1)S(1)} %get-tuple-element.50), channel_id=1, source_target_pairs={{0,16},{8,24},{16,0},{24,8},{1,17},{9,25},{17,1},{25,9},{2,18},{10... | collective-permute-start | bytes 786440 | tf_op jit(solution)/shard_map/ppermute | solution.py:224
  24.9 0.0 collective-permute-done.7.dk_in
  24.9 0.0 collective-permute-done.8.dv_in
  24.9 0.1 shard_map.89
  25.1 1.5 %collective-permute-start.9 = (bf16[2,64,256]{2,1,0:T(8,128)(2,1)S(1)}, bf16[2,64,256]{2,1,0:T(8,128)(2,1)S(1)}, u32[]{:S(2)}, u32[]{:S(2)}) collective-permute-start(bf16[2,64,256]{2,1,0:T(8,128)(2,1)S(1)} %get-tuple-element.56), channel_id=1, source_target_pairs={{0,1},{1,2},{2,3},{3,4},{4,5},{5,6},{6,7},{7,0},{8,9},{9,10},{10,1... | collective-permute-start | bytes 196616 | tf_op jit(solution)/shard_map/ppermute | solution.py:224
  26.6 1.6 %collective-permute-start.10 = (bf16[2,64,256]{2,1,0:T(8,128)(2,1)S(1)}, bf16[2,64,256]{2,1,0:T(8,128)(2,1)S(1)}, u32[]{:S(2)}, u32[]{:S(2)}) collective-permute-start(bf16[2,64,256]{2,1,0:T(8,128)(2,1)S(1)} %get-tuple-element.57), channel_id=1, source_target_pairs={{0,2},{1,3},{2,4},{3,5},{4,6},{5,7},{6,0},{7,1},{8,10},{9,11},{10,... | collective-permute-start | bytes 196616 | tf_op jit(solution)/shard_map/ppermute | solution.py:224
  28.2 2.6 %collective-permute-start.11 = (bf16[2,64,256]{2,1,0:T(8,128)(2,1)S(1)}, bf16[2,64,256]{2,1,0:T(8,128)(2,1)S(1)}, u32[]{:S(2)}, u32[]{:S(2)}) collective-permute-start(bf16[2,64,256]{2,1,0:T(8,128)(2,1)S(1)} %get-tuple-element.58), channel_id=1, source_target_pairs={{0,3},{1,4},{2,5},{3,6},{4,7},{5,0},{6,1},{7,2},{8,11},{9,12},{10,... | collective-permute-start | bytes 196616 | tf_op jit(solution)/shard_map/ppermute | solution.py:224
  30.8 1.2 %collective-permute-start.12 = (bf16[2,64,256]{2,1,0:T(8,128)(2,1)S(1)}, bf16[2,64,256]{2,1,0:T(8,128)(2,1)S(1)}, u32[]{:S(2)}, u32[]{:S(2)}) collective-permute-start(bf16[2,64,256]{2,1,0:T(8,128)(2,1)S(1)} %get-tuple-element.59), channel_id=1, source_target_pairs={{0,4},{1,5},{2,6},{3,7},{4,0},{5,1},{6,2},{7,3},{8,12},{9,13},{10,... | collective-permute-start | bytes 196616 | tf_op jit(solution)/shard_map/ppermute | solution.py:224
  32.0 0.0 collective-permute-done.6
  32.0 3.1 %collective-permute-start.13 = (bf16[2,64,256]{2,1,0:T(8,128)(2,1)S(1)}, bf16[2,64,256]{2,1,0:T(8,128)(2,1)S(1)}, u32[]{:S(2)}, u32[]{:S(2)}) collective-permute-start(bf16[2,64,256]{2,1,0:T(8,128)(2,1)S(1)} %get-tuple-element.60), channel_id=1, source_target_pairs={{0,5},{1,6},{2,7},{3,0},{4,1},{5,2},{6,3},{7,4},{8,13},{9,14},{10,... | collective-permute-start | bytes 196616 | tf_op jit(solution)/shard_map/ppermute | solution.py:224
  35.1 0.0 collective-permute-done.9
  35.1 1.3 %collective-permute-start.14 = (bf16[2,64,256]{2,1,0:T(8,128)(2,1)S(1)}, bf16[2,64,256]{2,1,0:T(8,128)(2,1)S(1)}, u32[]{:S(2)}, u32[]{:S(2)}) collective-permute-start(bf16[2,64,256]{2,1,0:T(8,128)(2,1)S(1)} %get-tuple-element.61), channel_id=1, source_target_pairs={{0,6},{1,7},{2,0},{3,1},{4,2},{5,3},{6,4},{7,5},{8,14},{9,15},{10,... | collective-permute-start | bytes 196616 | tf_op jit(solution)/shard_map/ppermute | solution.py:224
  36.5 0.0 collective-permute-done.10
  36.5 0.9 %collective-permute-start.15 = (bf16[2,64,256]{2,1,0:T(8,128)(2,1)S(1)}, bf16[2,64,256]{2,1,0:T(8,128)(2,1)S(1)}, u32[]{:S(2)}, u32[]{:S(2)}) collective-permute-start(bf16[2,64,256]{2,1,0:T(8,128)(2,1)S(1)} %get-tuple-element.62), channel_id=1, source_target_pairs={{0,7},{1,0},{2,1},{3,2},{4,3},{5,4},{6,5},{7,6},{8,15},{9,8},{10,9... | collective-permute-start | bytes 196616 | tf_op jit(solution)/shard_map/ppermute | solution.py:224
  37.4 0.8 %fusion = bf16[1,512,256]{2,1,0:T(8,128)(2,1)} fusion(f32[512,256]{1,0:T(8,128)S(1)} %get-tuple-element.49, bf16[512,256]{1,0:T(8,128)(2,1)S(1)} %collective-permute-done.6), kind=kLoop, calls=%fused_computation.1 | loop fusion | flops 524288 | bytes 1048576 | tf_op jit(solution)/shard_map/broadcast_in_dim | solution.py:327
  38.2 0.0 collective-permute-done.11
  38.2 0.0 collective-permute-done.12
  38.2 2.0 %collective-permute-done.13 = bf16[2,64,256]{2,1,0:T(8,128)(2,1)S(1)} collective-permute-done((bf16[2,64,256]{2,1,0:T(8,128)(2,1)S(1)}, bf16[2,64,256]{2,1,0:T(8,128)(2,1)S(1)}, u32[]{:S(2)}, u32[]{:S(2)}) %collective-permute-start.13) | collective-permute-done | bytes 65568 | tf_op jit(solution)/shard_map/ppermute | solution.py:224
  40.2 0.8 %collective-permute-done.14 = bf16[2,64,256]{2,1,0:T(8,128)(2,1)S(1)} collective-permute-done((bf16[2,64,256]{2,1,0:T(8,128)(2,1)S(1)}, bf16[2,64,256]{2,1,0:T(8,128)(2,1)S(1)}, u32[]{:S(2)}, u32[]{:S(2)}) %collective-permute-start.14) | collective-permute-done | bytes 65568 | tf_op jit(solution)/shard_map/ppermute | solution.py:224
  41.0 0.0 collective-permute-done.15
  41.0 0.1 convert_add_fusion
  41.1 0.7 %fusion.1 = (f32[1,64,256]{2,1,0:T(8,128)}, f32[1,64,256]{2,1,0:T(8,128)}) fusion(f32[2,64,256]{2,1,0:T(8,128)S(1)} %convert_add_fusion), kind=kLoop, calls=%fused_computation.3 | loop fusion | bytes 262144 | tf_op jit(solution)/shard_map/slice | solution.py:341
Async XLA Ops:
  0.6 9.4 %collective-permute-start = (bf16[512,256]{1,0:T(8,128)(2,1)}, bf16[512,256]{1,0:T(8,128)(2,1)S(1)}, u32[]{:S(2)}, u32[]{:S(2)}) collective-permute-start(bf16[512,256]{1,0:T(8,128)(2,1)} %bitcast.6), channel_id=1, source_target_pairs={{0,8},{8,0},{16,24},{24,16},{1,9},{9,1},{17,25},{25,17},{2,10},{10... | collective-permute-start | bytes 786440 | tf_op jit(solution)/shard_map/ppermute | solution.py:228
  1.2 8.8 %collective-permute-start.1 = (bf16[512,256]{1,0:T(8,128)(2,1)}, bf16[512,256]{1,0:T(8,128)(2,1)S(1)}, u32[]{:S(2)}, u32[]{:S(2)}) collective-permute-start(bf16[512,256]{1,0:T(8,128)(2,1)} %bitcast.8), channel_id=1, source_target_pairs={{0,8},{8,0},{16,24},{24,16},{1,9},{9,1},{17,25},{25,17},{2,10},{10... | collective-permute-start | bytes 786440 | tf_op jit(solution)/shard_map/ppermute | solution.py:228
  1.3 12.1 %collective-permute-start.2 = (bf16[512,256]{1,0:T(8,128)(2,1)}, bf16[512,256]{1,0:T(8,128)(2,1)S(1)}, u32[]{:S(2)}, u32[]{:S(2)}) collective-permute-start(bf16[512,256]{1,0:T(8,128)(2,1)} %bitcast.10), channel_id=1, source_target_pairs={{0,16},{8,24},{16,0},{24,8},{1,17},{9,25},{17,1},{25,9},{2,18},{10... | collective-permute-start | bytes 786440 | tf_op jit(solution)/shard_map/ppermute | solution.py:224
  4.2 12.5 %collective-permute-start.3 = (bf16[512,256]{1,0:T(8,128)(2,1)}, bf16[512,256]{1,0:T(8,128)(2,1)S(1)}, u32[]{:S(2)}, u32[]{:S(2)}) collective-permute-start(bf16[512,256]{1,0:T(8,128)(2,1)} %bitcast.12), channel_id=1, source_target_pairs={{0,16},{8,24},{16,0},{24,8},{1,17},{9,25},{17,1},{25,9},{2,18},{10... | collective-permute-start | bytes 786440 | tf_op jit(solution)/shard_map/ppermute | solution.py:224
  4.2 0.9 %copy-start = (bf16[1,512,256]{2,1,0:T(8,128)(2,1)S(1)}, bf16[1,512,256]{2,1,0:T(8,128)(2,1)}, u32[]{:S(2)}) copy-start(bf16[1,512,256]{2,1,0:T(8,128)(2,1)} %param.7) | copy-start | bytes 786436
  5.2 0.9 %copy-start.1 = (bf16[1,512,256]{2,1,0:T(8,128)(2,1)S(1)}, bf16[1,512,256]{2,1,0:T(8,128)(2,1)}, u32[]{:S(2)}) copy-start(bf16[1,512,256]{2,1,0:T(8,128)(2,1)} %param.8) | copy-start | bytes 786436
  6.1 0.9 %copy-start.2 = (bf16[1,512,256]{2,1,0:T(8,128)(2,1)S(1)}, bf16[1,512,256]{2,1,0:T(8,128)(2,1)}, u32[]{:S(2)}) copy-start(bf16[1,512,256]{2,1,0:T(8,128)(2,1)} %param.6) | copy-start | bytes 786436
  7.1 0.9 %copy-start.3 = (bf16[1,512,256]{2,1,0:T(8,128)(2,1)S(1)}, bf16[1,512,256]{2,1,0:T(8,128)(2,1)}, u32[]{:S(2)}) copy-start(bf16[1,512,256]{2,1,0:T(8,128)(2,1)} %param.9) | copy-start | bytes 786436
  8.0 0.7 %copy-start.4 = (s32[1,8]{1,0:T(1,128)S(1)}, s32[1,8]{1,0:T(1,128)}, u32[]{:S(2)}) copy-start(s32[1,8]{1,0:T(1,128)} %docs.1) | copy-start | bytes 100
  8.7 0.7 %copy-start.5 = (s32[8]{0:T(128)S(1)}, s32[8]{0:T(128)}, u32[]{:S(2)}) copy-start(s32[8]{0:T(128)} %fold.1) | copy-start | bytes 100
  11.6 7.8 %collective-permute-start.5 = (f32[3,512]{1,0:T(4,128)S(1)}, f32[3,512]{1,0:T(4,128)S(1)}, u32[]{:S(2)}, u32[]{:S(2)}) collective-permute-start(f32[3,512]{1,0:T(4,128)S(1)} %get-tuple-element.41.refs_2_), channel_id=1, source_target_pairs={{0,16},{8,24},{16,0},{24,8},{1,17},{9,25},{17,1},{25,9},{2,18},{10... | collective-permute-start | bytes 18440 | tf_op jit(solution)/shard_map/ppermute | solution.py:224
  17.3 3.8 %collective-permute-start.4 = (f32[3,512]{1,0:T(4,128)S(1)}, f32[3,512]{1,0:T(4,128)S(1)}, u32[]{:S(2)}, u32[]{:S(2)}) collective-permute-start(f32[3,512]{1,0:T(4,128)S(1)} %get-tuple-element.44.refs_2_), channel_id=1, source_target_pairs={{0,16},{8,24},{16,0},{24,8},{1,17},{9,25},{17,1},{25,9},{2,18},{10... | collective-permute-start | bytes 18440 | tf_op jit(solution)/shard_map/ppermute | solution.py:224
  22.6 2.4 %collective-permute-start.7 = (bf16[512,256]{1,0:T(8,128)(2,1)S(1)}, bf16[512,256]{1,0:T(8,128)(2,1)S(1)}, u32[]{:S(2)}, u32[]{:S(2)}) collective-permute-start(bf16[512,256]{1,0:T(8,128)(2,1)S(1)} %get-tuple-element.53), channel_id=1, source_target_pairs={{0,8},{8,0},{16,24},{24,16},{1,9},{9,1},{17,25},{25,17},{2,10},{10... | collective-permute-start | bytes 786440 | tf_op jit(solution)/shard_map/ppermute | solution.py:228
  22.7 2.3 %collective-permute-start.8 = (bf16[512,256]{1,0:T(8,128)(2,1)S(1)}, bf16[512,256]{1,0:T(8,128)(2,1)S(1)}, u32[]{:S(2)}, u32[]{:S(2)}) collective-permute-start(bf16[512,256]{1,0:T(8,128)(2,1)S(1)} %get-tuple-element.54), channel_id=1, source_target_pairs={{0,8},{8,0},{16,24},{24,16},{1,9},{9,1},{17,25},{25,17},{2,10},{10... | collective-permute-start | bytes 786440 | tf_op jit(solution)/shard_map/ppermute | solution.py:228
  23.2 8.8 %collective-permute-start.6 = (bf16[512,256]{1,0:T(8,128)(2,1)S(1)}, bf16[512,256]{1,0:T(8,128)(2,1)S(1)}, u32[]{:S(2)}, u32[]{:S(2)}) collective-permute-start(bf16[512,256]{1,0:T(8,128)(2,1)S(1)} %get-tuple-element.50), channel_id=1, source_target_pairs={{0,16},{8,24},{16,0},{24,8},{1,17},{9,25},{17,1},{25,9},{2,18},{10... | collective-permute-start | bytes 786440 | tf_op jit(solution)/shard_map/ppermute | solution.py:224
  25.1 10.0 %collective-permute-start.9 = (bf16[2,64,256]{2,1,0:T(8,128)(2,1)S(1)}, bf16[2,64,256]{2,1,0:T(8,128)(2,1)S(1)}, u32[]{:S(2)}, u32[]{:S(2)}) collective-permute-start(bf16[2,64,256]{2,1,0:T(8,128)(2,1)S(1)} %get-tuple-element.56), channel_id=1, source_target_pairs={{0,1},{1,2},{2,3},{3,4},{4,5},{5,6},{6,7},{7,0},{8,9},{9,10},{10,1... | collective-permute-start | bytes 196616 | tf_op jit(solution)/shard_map/ppermute | solution.py:224
  26.6 9.9 %collective-permute-start.10 = (bf16[2,64,256]{2,1,0:T(8,128)(2,1)S(1)}, bf16[2,64,256]{2,1,0:T(8,128)(2,1)S(1)}, u32[]{:S(2)}, u32[]{:S(2)}) collective-permute-start(bf16[2,64,256]{2,1,0:T(8,128)(2,1)S(1)} %get-tuple-element.57), channel_id=1, source_target_pairs={{0,2},{1,3},{2,4},{3,5},{4,6},{5,7},{6,0},{7,1},{8,10},{9,11},{10,... | collective-permute-start | bytes 196616 | tf_op jit(solution)/shard_map/ppermute | solution.py:224
  28.2 10.0 %collective-permute-start.11 = (bf16[2,64,256]{2,1,0:T(8,128)(2,1)S(1)}, bf16[2,64,256]{2,1,0:T(8,128)(2,1)S(1)}, u32[]{:S(2)}, u32[]{:S(2)}) collective-permute-start(bf16[2,64,256]{2,1,0:T(8,128)(2,1)S(1)} %get-tuple-element.58), channel_id=1, source_target_pairs={{0,3},{1,4},{2,5},{3,6},{4,7},{5,0},{6,1},{7,2},{8,11},{9,12},{10,... | collective-permute-start | bytes 196616 | tf_op jit(solution)/shard_map/ppermute | solution.py:224
  30.8 7.4 %collective-permute-start.12 = (bf16[2,64,256]{2,1,0:T(8,128)(2,1)S(1)}, bf16[2,64,256]{2,1,0:T(8,128)(2,1)S(1)}, u32[]{:S(2)}, u32[]{:S(2)}) collective-permute-start(bf16[2,64,256]{2,1,0:T(8,128)(2,1)S(1)} %get-tuple-element.59), channel_id=1, source_target_pairs={{0,4},{1,5},{2,6},{3,7},{4,0},{5,1},{6,2},{7,3},{8,12},{9,13},{10,... | collective-permute-start | bytes 196616 | tf_op jit(solution)/shard_map/ppermute | solution.py:224
  32.0 8.2 %collective-permute-start.13 = (bf16[2,64,256]{2,1,0:T(8,128)(2,1)S(1)}, bf16[2,64,256]{2,1,0:T(8,128)(2,1)S(1)}, u32[]{:S(2)}, u32[]{:S(2)}) collective-permute-start(bf16[2,64,256]{2,1,0:T(8,128)(2,1)S(1)} %get-tuple-element.60), channel_id=1, source_target_pairs={{0,5},{1,6},{2,7},{3,0},{4,1},{5,2},{6,3},{7,4},{8,13},{9,14},{10,... | collective-permute-start | bytes 196616 | tf_op jit(solution)/shard_map/ppermute | solution.py:224
  35.1 5.9 %collective-permute-start.14 = (bf16[2,64,256]{2,1,0:T(8,128)(2,1)S(1)}, bf16[2,64,256]{2,1,0:T(8,128)(2,1)S(1)}, u32[]{:S(2)}, u32[]{:S(2)}) collective-permute-start(bf16[2,64,256]{2,1,0:T(8,128)(2,1)S(1)} %get-tuple-element.61), channel_id=1, source_target_pairs={{0,6},{1,7},{2,0},{3,1},{4,2},{5,3},{6,4},{7,5},{8,14},{9,15},{10,... | collective-permute-start | bytes 196616 | tf_op jit(solution)/shard_map/ppermute | solution.py:224
  36.5 4.6 %collective-permute-start.15 = (bf16[2,64,256]{2,1,0:T(8,128)(2,1)S(1)}, bf16[2,64,256]{2,1,0:T(8,128)(2,1)S(1)}, u32[]{:S(2)}, u32[]{:S(2)}) collective-permute-start(bf16[2,64,256]{2,1,0:T(8,128)(2,1)S(1)} %get-tuple-element.62), channel_id=1, source_target_pairs={{0,7},{1,0},{2,1},{3,2},{4,3},{5,4},{6,5},{7,6},{8,15},{9,8},{10,9... | collective-permute-start | bytes 196616 | tf_op jit(solution)/shard_map/ppermute | solution.py:224

commit v4 on v3

--- a/solution.py
+++ b/solution.py
@@ -13,6 +13,7 @@
 MASKED = -1e30
 VMEM_LIMIT = 14 * 1024 * 1024
 CORES = 2
+MINOR = 2
 
 
 def contract(left, right, left_dim, right_dim):
@@ -186,19 +187,31 @@
                 settle(False, query_target, query_source, None)
 
 
-def split_body(scaling, order, dk, dv, dk_in, dv_in, *outs):
+def split_values(dv, dv_in, keep, send):
     head = lax.axis_index("head")
-    piece = outs[0].shape[1]
-    for step, out in zip([0] + order, outs):
-        rows = pl.ds(pl.multiple_of(lax.rem(head + step, lax.axis_size("head")) * piece, piece), piece)
-        key_sum = (dk[rows, :] + dk_in[rows, :].astype(jnp.float32)) * scaling
-        value_sum = dv[rows, :] + dv_in[rows, :].astype(jnp.float32)
-        out[0] = key_sum.astype(out.dtype)
-        out[1] = value_sum.astype(out.dtype)
-
-
-def exchange_order(heads):
-    return list(range(1, heads))
+    member = lax.rem(head, MINOR)
+    piece = keep.shape[1]
+    for g in range(keep.shape[0]):
+        for out, m in ((keep, member), (send, member ^ 1)):
+            rows = pl.ds(pl.multiple_of((g * MINOR + m) * piece, piece), piece)
+            total = dv[rows, :] + dv_in[rows, :].astype(jnp.float32)
+            out[g] = total.astype(out.dtype)
+
+
+def split_keys(scaling, steps, dk, dk_in, *outs):
+    group = lax.axis_index("head") // MINOR
+    rows_each = outs[0].shape[0]
+    for step, out in zip([0] + steps, outs):
+        rows = pl.ds(pl.multiple_of((group ^ step) * rows_each, rows_each), rows_each)
+        total = (dk[rows, :] + dk_in[rows, :].astype(jnp.float32)) * scaling
+        out[...] = total.astype(out.dtype)
+
+
+def values_body(steps, value_keep, value_in, *outs):
+    group = lax.axis_index("head") // MINOR
+    for step, out in zip([0] + steps, outs):
+        total = value_keep[group ^ step] + value_in[group ^ step].astype(jnp.float32)
+        out[...] = total.astype(out.dtype)
 
 
 def by_row(row_count, steps, terms):
@@ -206,15 +219,37 @@
     rows = []
     for r in range(row_count):
         total = None
-        for step, term in zip(steps, terms):
-            term = term.astype(jnp.float32)
+        for step, term in zip([0] + steps, terms):
+            term = term[...].astype(jnp.float32)
             if row_count > 1:
-                term = jnp.where(lax.rem(head - step + lax.axis_size("head"), lax.axis_size("head")) // HEAD_COUNT == r, term, 0.0)
+                term = jnp.where((head ^ (step * MINOR)) // HEAD_COUNT == r, term, 0.0)
             total = term if total is None else total + term
         rows.append(total)
     return rows
 
 
+def keys_body(row_count, steps, *refs):
+    terms, (keep, send) = refs[:-2], refs[-2:]
+    member = lax.rem(lax.axis_index("head"), MINOR)
+    piece = keep.shape[1]
+    for r, total in enumerate(by_row(row_count, steps, terms)):
+        first, second = total[:piece], total[piece:]
+        keep[r] = jnp.where(member == 0, first, second)
+        send[r] = jnp.where(member == 0, second, first).astype(send.dtype)
+
+
+def finish_body(row_count, steps, key_mine, key_in, *refs):
+    terms, (grad_keys, grad_values) = refs[:-2], refs[-2:]
+    grad_keys[...] = key_mine[...] + key_in[...].astype(jnp.float32)
+    for r, total in enumerate(by_row(row_count, steps, terms)):
+        grad_values[r] = total
+
+
+def major_steps(heads):
+    major = heads // MINOR
+    return sorted(range(1, major), key=lambda step: (-(step & (major // 2)), step))
+
+
 SMEM = pl.BlockSpec(memory_space=pltpu.SMEM)
 VMEM = pl.BlockSpec(memory_space=pltpu.VMEM)
 
@@ -222,6 +257,11 @@
 def shift(x, axis, amount):
     size = lax.axis_size(axis)
     return lax.ppermute(x, axis, [(i, (i - amount) % size) for i in range(size)])
+
+
+def swap(x, bits):
+    size = lax.axis_size("head")
+    return lax.ppermute(x, "head", [(i, i ^ bits) for i in range(size)])
 
 
 def swap_cores(x):
@@ -246,6 +286,7 @@
     local, width = queries.shape[1:]
     chips = lax.axis_size("seq") // CORES
     heads = lax.axis_size("head")
+    major = heads // MINOR
     row_count = keys.shape[0]
     piece = local // heads
     block = local // (fold_order.shape[0] // lax.axis_size("seq"))
@@ -311,14 +352,16 @@
         results = kernel(
             functools.partial(grads_body, chips, first, last),
             (*held[offset], *sets[offset], key_own, key_sib, *parts, *acc),
-            [mine if offset == 0 else sent] + ([mine, mine, sent, sent] if last else [wide, wide]),
+            [mine if offset == 0 else sent]
+            + ([mine, mine, sent, sent] if last else [wide, wide]),
             1.5 * work,
             [pltpu.VMEM((CORES * local, width), full)] * 2 + [pltpu.VMEM((block, width), full)],
         )
         partial_queries[offset] = results[0]
         acc = results[1:]
     dk, dv, dk_out, dv_out = acc
-    dk_in, dv_in = swap_cores(dk_out), swap_cores(dv_out)
+    dv_in = swap_cores(dv_out)
+    dk_in = swap_cores(dk_out)
     grad_query = partial_queries[0]
     for offset in range(1, chips):
         grad_query = grad_query + shift(
@@ -326,19 +369,48 @@
         ).astype(full)
     grad_queries = (grad_query * scaling).astype(low)[None]
 
-    order = exchange_order(heads)
-    moved = kernel(
-        functools.partial(split_body, scaling, order),
-        (dk, dv, dk_in, dv_in),
-        [shape((2, piece, width), full)] + [shape((2, piece, width), low)] * (heads - 1),
-        4 * local * width,
-    )
-    terms = [moved[0]]
-    for step, x in zip(order, moved[1:]):
-        terms.append(shift(x, "head", -step))
-    rows = by_row(row_count, [0] + order, terms)
-    grad_keys = jnp.stack([total[0] for total in rows])
-    grad_values = jnp.stack([total[1] for total in rows])
+    tail = 4 * local * width
+    steps = major_steps(heads)
+    value_keep, value_send = kernel(
+        split_values,
+        (dv, dv_in),
+        [shape((major, piece, width), full), shape((major, piece, width), low)],
+        tail,
+    )
+    value_in = swap(value_send, 1)
+    key_keep, *key_send = kernel(
+        functools.partial(split_keys, scaling, steps),
+        (dk, dk_in),
+        [shape((MINOR * piece, width), full)]
+        + [shape((MINOR * piece, width), low)] * (major - 1),
+        tail,
+    )
+    key_terms = [key_keep]
+    for step, x in zip(steps, key_send):
+        key_terms.append(swap(x, step * MINOR))
+    value_mine, *value_out = kernel(
+        functools.partial(values_body, steps),
+        (value_keep, value_in),
+        [shape((piece, width), full)] + [shape((piece, width), low)] * (major - 1),
+        tail,
+    )
+    value_terms = [value_mine]
+    for step, x in zip(steps, value_out):
+        value_terms.append(swap(x, step * MINOR))
+    owned = (row_count, piece, width)
+    key_mine, key_out = kernel(
+        functools.partial(keys_body, row_count, steps),
+        key_terms,
+        [shape(owned, full), shape(owned, low)],
+        tail,
+    )
+    key_in = swap(key_out, 1)
+    grad_keys, grad_values = kernel(
+        functools.partial(finish_body, row_count, steps),
+        (key_mine, key_in, *value_terms),
+        [shape(owned, full)] * 2,
+        tail,
+    )
     return grad_queries, grad_keys, grad_values
 
 

time: 42 us -> 45.3 us (1.079)
  waiting for transfers between devices: 6.99 us -> 12.6 us
  starting transfers between devices: 22.1 us -> 19.8 us
  Pallas kernels: 5.33 us -> 6.05 us
  local copies, waits for them, and re-layouts: 5.77 us -> 5.11 us
    ppermute x12 -> x5, starting transfers between devices: 20.9 us -> 8.61 us  [shift(): lax.ppermute(x, axis, [(i, (i - amount) % size) for i in range(size)])]
    ppermute x0 -> x8, starting transfers between devices: none -> 9.95 us  [swap(): return lax.ppermute(x, 'head', [(i, i ^ bits) for i in range(size)])]
    ppermute x0 -> x8, waiting for transfers between devices: none -> 8.5 us  [swap(): return lax.ppermute(x, 'head', [(i, i ^ bits) for i in range(size)])]
    ppermute x12 -> x5, waiting for transfers between devices: 6.98 us -> 4.11 us  [shift(): lax.ppermute(x, axis, [(i, (i - amount) % size) for i in range(size)])]
    pallas_call x5 -> x9, Pallas kernels: 4.69 us -> 5.41 us  [kernel(): pl.pallas_call(body, out_shape=outs, in_specs=[SMEM if x.dtype == jnp.int...]
    slice x1 -> x0, local copies, waits for them, and re-layouts: 0.66 us -> none  [gradients(): grad_values = jnp.stack([total[1] for total in rows])]
  transfers between devices with their start and end apart: 16 -> 17, of which waited for: 4 -> 7; matrix products, arithmetic and copies ran while one was open for 2% -> 2% of each run, Pallas kernels for 9% -> 9%
where the time goes in v4:
time: 45.3 us; the launch traced here: 45 us
  starting transfers between devices  19.8 us (44%)
  waiting for transfers between devices  12.6 us (28%)
  Pallas kernels  6.05 us (13%)
  local copies, waits for them, and re-layouts  5.11 us (11%)
  other arithmetic  0.77 us (2%)
  between operations  0.73 us (2%)
    ppermute x8, starting transfers between devices, swap(): return lax.ppermute(x, 'head', [(i, i ^ bits) for i in range(size)])  9.95 us
    ppermute x5, starting transfers between devices, shift(): lax.ppermute(x, axis, [(i, (i - amount) % size) for i in range(size)])  8.61 us
    ppermute x8, waiting for transfers between devices, swap(): return lax.ppermute(x, 'head', [(i, i ^ bits) for i in range(size)])  8.5 us
    pallas_call x9, Pallas kernels, kernel(): pl.pallas_call(body, out_shape=outs, in_specs=[SMEM if x.dtype == jnp.int...  5.41 us
    unnamed x12, local copies, waits for them, and re-layouts  5.11 us
    ppermute x5, waiting for transfers between devices, shift(): lax.ppermute(x, axis, [(i, (i - amount) % size) for i in range(size)])  4.11 us
    ppermute x4, starting transfers between devices, swap_cores(): lax.ppermute(x, 'seq', [(i, i ^ 1) for i in range(lax.axis_size('seq'))])  1.2 us
  transfers between devices with their start and end apart: 17, of which 7 were waited for; matrix products, arithmetic and copies ran while one was open for 2% of the time, Pallas kernels for 9%

profile of v4, /device:TPU:0, one launch (start us, length us, event | category | flops | bytes accessed | tf_op | source)
XLA Modules:
  0.0 45.0 jit_solution(2332246928258789774)
XLA Ops:
  0.6 0.6 %collective-permute-start = (bf16[512,256]{1,0:T(8,128)(2,1)}, bf16[512,256]{1,0:T(8,128)(2,1)S(1)}, u32[]{:S(2)}, u32[]{:S(2)}) collective-permute-start(bf16[512,256]{1,0:T(8,128)(2,1)} %bitcast.6), channel_id=1, source_target_pairs={{0,8},{8,0},{16,24},{24,16},{1,9},{9,1},{17,25},{25,17},{2,10},{10... | collective-permute-start | bytes 786440 | tf_op jit(solution)/shard_map/ppermute | solution.py:268
  1.2 0.1 collective-permute-start.1
  1.3 2.9 %collective-permute-start.2 = (bf16[512,256]{1,0:T(8,128)(2,1)}, bf16[512,256]{1,0:T(8,128)(2,1)S(1)}, u32[]{:S(2)}, u32[]{:S(2)}) collective-permute-start(bf16[512,256]{1,0:T(8,128)(2,1)} %bitcast.10), channel_id=1, source_target_pairs={{0,16},{8,24},{16,0},{24,8},{1,17},{9,25},{17,1},{25,9},{2,18},{10... | collective-permute-start | bytes 786440 | tf_op jit(solution)/shard_map/ppermute | solution.py:259
  4.2 0.0 collective-permute-start.3
  4.2 0.0 copy-start
  4.2 0.9 %copy-done = bf16[1,512,256]{2,1,0:T(8,128)(2,1)S(1)} copy-done((bf16[1,512,256]{2,1,0:T(8,128)(2,1)S(1)}, bf16[1,512,256]{2,1,0:T(8,128)(2,1)}, u32[]{:S(2)}) %copy-start) | copy-done | bytes 262168
  5.2 0.0 copy-start.1
  5.2 0.9 %copy-done.1 = bf16[1,512,256]{2,1,0:T(8,128)(2,1)S(1)} copy-done((bf16[1,512,256]{2,1,0:T(8,128)(2,1)S(1)}, bf16[1,512,256]{2,1,0:T(8,128)(2,1)}, u32[]{:S(2)}) %copy-start.1) | copy-done | bytes 262168
  6.1 0.0 copy-start.2
  6.1 0.9 %copy-done.2 = bf16[1,512,256]{2,1,0:T(8,128)(2,1)S(1)} copy-done((bf16[1,512,256]{2,1,0:T(8,128)(2,1)S(1)}, bf16[1,512,256]{2,1,0:T(8,128)(2,1)}, u32[]{:S(2)}) %copy-start.2) | copy-done | bytes 262168
  7.1 0.0 copy-start.3
  7.1 0.9 %copy-done.3 = bf16[1,512,256]{2,1,0:T(8,128)(2,1)S(1)} copy-done((bf16[1,512,256]{2,1,0:T(8,128)(2,1)S(1)}, bf16[1,512,256]{2,1,0:T(8,128)(2,1)}, u32[]{:S(2)}) %copy-start.3) | copy-done | bytes 262168
  8.0 0.0 copy-start.4
  8.0 0.7 %copy-done.4 = s32[1,8]{1,0:T(1,128)S(1)} copy-done((s32[1,8]{1,0:T(1,128)S(1)}, s32[1,8]{1,0:T(1,128)}, u32[]{:S(2)}) %copy-start.4) | copy-done | bytes 56
  8.7 0.0 copy-start.5
  8.7 0.7 %copy-done.5 = s32[8]{0:T(128)S(1)} copy-done((s32[8]{0:T(128)S(1)}, s32[8]{0:T(128)}, u32[]{:S(2)}) %copy-start.5) | copy-done | bytes 56
  9.3 0.6 %place.1 = (bf16[512,256]{1,0:T(8,128)(2,1)S(1)}, bf16[512,256]{1,0:T(8,128)(2,1)S(1)}, bf16[512,256]{1,0:T(8,128)(2,1)S(1)}, bf16[512,256]{1,0:T(8,128)(2,1)S(1...) custom-call(s32[1,8]{1,0:T(1,128)S(1)} %copy-done.4, ...), custom_call_target="tpu_custom_call" | custom-call | flops 1048576 | bytes 16384 | tf_op jit(solution)/shard_map/place/pallas_call | solution.py:313
  10.0 0.0 collective-permute-done.refs_1_
  10.0 0.0 collective-permute-done.1.refs_3_
  10.0 1.6 %shard_map.85 = (f32[3,512]{1,0:T(4,128)S(1)}, f32[1024,512]{1,0:T(8,128)S(1)}, f32[1024,512]{1,0:T(8,128)S(1)}) custom-call(s32[16,256]{1,0:T(8,128)S(1)} %get-tuple-element.40.info, s32[8,128]{1,0:T(8,128)S(1)} %get-tuple-element.39.word, bf16[512,256]{1,0:T(8,128)(2,1)S(1)} %get-tuple-element.41.query, bf16[512,256]{1,0:T(8,128)(2,1)S(1)} %get-tuple-element.42.grad, ...), custom_call_target="tpu_custom_call" | custom-call | flops 536870912 | bytes 2097152 | tf_op jit(solution)/shard_map/pallas_call | solution.py:272
  11.6 1.7 %collective-permute-start.5 = (f32[3,512]{1,0:T(4,128)S(1)}, f32[3,512]{1,0:T(4,128)S(1)}, u32[]{:S(2)}, u32[]{:S(2)}) collective-permute-start(f32[3,512]{1,0:T(4,128)S(1)} %get-tuple-element.47.refs_2_), channel_id=1, source_target_pairs={{0,16},{8,24},{16,0},{24,8},{1,17},{9,25},{17,1},{25,9},{2,18},{10... | collective-permute-start | bytes 18440 | tf_op jit(solution)/shard_map/ppermute | solution.py:259
  13.3 0.0 collective-permute-done.2.query
  13.4 3.3 %collective-permute-done.3.grad = bf16[512,256]{1,0:T(8,128)(2,1)S(1)} collective-permute-done((bf16[512,256]{1,0:T(8,128)(2,1)}, bf16[512,256]{1,0:T(8,128)(2,1)S(1)}, u32[]{:S(2)}, u32[]{:S(2)}) %collective-permute-start.3) | collective-permute-done | bytes 262176 | tf_op jit(solution)/shard_map/ppermute | solution.py:259
  16.7 0.6 %shard_map.86 = (f32[3,512]{1,0:T(4,128)S(1)}, f32[1024,512]{1,0:T(8,128)S(1)}, f32[1024,512]{1,0:T(8,128)S(1)}) custom-call(s32[16,256]{1,0:T(8,128)S(1)} %get-tuple-element.48.info, s32[8,128]{1,0:T(8,128)S(1)} %get-tuple-element.49.word, bf16[512,256]{1,0:T(8,128)(2,1)S(1)} %collective-permute-done.2.query, ...), custom_call_target="tpu_custom_call" | custom-call | flops 536870912 | bytes 2097152 | tf_op jit(solution)/shard_map/pallas_call | solution.py:272
  17.3 2.1 %collective-permute-start.4 = (f32[3,512]{1,0:T(4,128)S(1)}, f32[3,512]{1,0:T(4,128)S(1)}, u32[]{:S(2)}, u32[]{:S(2)}) collective-permute-start(f32[3,512]{1,0:T(4,128)S(1)} %get-tuple-element.50.refs_2_), channel_id=1, source_target_pairs={{0,16},{8,24},{16,0},{24,8},{1,17},{9,25},{17,1},{25,9},{2,18},{10... | collective-permute-start | bytes 18440 | tf_op jit(solution)/shard_map/ppermute | solution.py:259
  19.4 0.0 collective-permute-done.5.refs_3_
  19.4 0.8 %shard_map.87 = (bf16[512,256]{1,0:T(8,128)(2,1)S(1)}, f32[1024,256]{1,0:T(8,128)S(1)}, f32[1024,256]{1,0:T(8,128)S(1)}) custom-call(s32[8,128]{1,0:T(8,128)S(1)} %get-tuple-element.49.word, f32[1024,512]{1,0:T(8,128)S(1)} %get-tuple-element.51.scores, f32[1024,512]{1,0:T(8,128)S(1)} %get-tuple-element.52.probs, ...), custom_call_target="tpu_custom_call" | custom-call | flops 805306368 | bytes 3145728 | tf_op jit(solution)/shard_map/pallas_call | solution.py:272
  20.2 0.8 %collective-permute-done.4.refs_3_ = f32[3,512]{1,0:T(4,128)S(1)} collective-permute-done((f32[3,512]{1,0:T(4,128)S(1)}, f32[3,512]{1,0:T(4,128)S(1)}, u32[]{:S(2)}, u32[]{:S(2)}) %collective-permute-start.4) | collective-permute-done | bytes 6176 | tf_op jit(solution)/shard_map/ppermute | solution.py:259
  21.0 1.6 %shard_map.88 = (f32[512,256]{1,0:T(8,128)S(1)}, f32[512,256]{1,0:T(8,128)S(1)}, f32[512,256]{1,0:T(8,128)S(1)}, bf16[512,256]{1,0:T(8,128)(2,1)S(1)}, bf16[512,256]{1,0:T(8,128)(2,1)S(1)}) custom-call(s32[8,128]{1,0:T(8,128)S(1)} %get-tuple-element.39.word, f32[1024,512]{1,0:T(8,128)S(1)} %get-tuple-element.45.scores, ...), custom_call_target="tpu_custom_call" | custom-call | flops 805306368 | bytes 3145728 | tf_op jit(solution)/shard_map/pallas_call | solution.py:272
  22.6 0.1 collective-permute-start.12
  22.7 0.5 %collective-permute-start.7 = (bf16[512,256]{1,0:T(8,128)(2,1)S(1)}, bf16[512,256]{1,0:T(8,128)(2,1)S(1)}, u32[]{:S(2)}, u32[]{:S(2)}) collective-permute-start(bf16[512,256]{1,0:T(8,128)(2,1)S(1)} %get-tuple-element.58), channel_id=1, source_target_pairs={{0,8},{8,0},{16,24},{24,16},{1,9},{9,1},{17,25},{25,17},{2,10},{10... | collective-permute-start | bytes 786440 | tf_op jit(solution)/shard_map/ppermute | solution.py:268
  23.2 1.8 %collective-permute-start.6 = (bf16[512,256]{1,0:T(8,128)(2,1)S(1)}, bf16[512,256]{1,0:T(8,128)(2,1)S(1)}, u32[]{:S(2)}, u32[]{:S(2)}) collective-permute-start(bf16[512,256]{1,0:T(8,128)(2,1)S(1)} %get-tuple-element.56), channel_id=1, source_target_pairs={{0,16},{8,24},{16,0},{24,8},{1,17},{9,25},{17,1},{25,9},{2,18},{10... | collective-permute-start | bytes 786440 | tf_op jit(solution)/shard_map/ppermute | solution.py:259
  24.9 0.0 collective-permute-done.12.dv_in
  24.9 0.1 shard_map.91
  25.0 1.6 %collective-permute-start.13 = (bf16[4,64,256]{2,1,0:T(8,128)(2,1)S(1)}, bf16[4,64,256]{2,1,0:T(8,128)(2,1)S(1)}, u32[]{:S(2)}, u32[]{:S(2)}) collective-permute-start(bf16[4,64,256]{2,1,0:T(8,128)(2,1)S(1)} %get-tuple-element.68), channel_id=1, source_target_pairs={{0,1},{1,0},{2,3},{3,2},{4,5},{5,4},{6,7},{7,6},{8,9},{9,8},{10,11... | collective-permute-start | bytes 393224 | tf_op jit(solution)/shard_map/ppermute | solution.py:264
  26.6 0.0 collective-permute-done.7.dk_in
  26.6 0.1 shard_map.89
  26.6 2.7 %collective-permute-start.8 = (bf16[128,256]{1,0:T(8,128)(2,1)S(1)}, bf16[128,256]{1,0:T(8,128)(2,1)S(1)}, u32[]{:S(2)}, u32[]{:S(2)}) collective-permute-start(bf16[128,256]{1,0:T(8,128)(2,1)S(1)} %get-tuple-element.60), channel_id=1, source_target_pairs={{0,4},{1,5},{2,6},{3,7},{4,0},{5,1},{6,2},{7,3},{8,12},{9,13},{10,... | collective-permute-start | bytes 196616 | tf_op jit(solution)/shard_map/ppermute | solution.py:264
  29.3 1.4 %collective-permute-start.9 = (bf16[128,256]{1,0:T(8,128)(2,1)S(1)}, bf16[128,256]{1,0:T(8,128)(2,1)S(1)}, u32[]{:S(2)}, u32[]{:S(2)}) collective-permute-start(bf16[128,256]{1,0:T(8,128)(2,1)S(1)} %get-tuple-element.61), channel_id=1, source_target_pairs={{0,6},{1,7},{2,4},{3,5},{4,2},{5,3},{6,0},{7,1},{8,14},{9,15},{10,... | collective-permute-start | bytes 196616 | tf_op jit(solution)/shard_map/ppermute | solution.py:264
  30.6 0.2 collective-permute-start.10
  30.9 1.3 %collective-permute-done.8.refs_1_ = bf16[128,256]{1,0:T(8,128)(2,1)S(1)} collective-permute-done((bf16[128,256]{1,0:T(8,128)(2,1)S(1)}, bf16[128,256]{1,0:T(8,128)(2,1)S(1)}, u32[]{:S(2)}, u32[]{:S(2)}) %collective-permute-start.8) | collective-permute-done | bytes 65568 | tf_op jit(solution)/shard_map/ppermute | solution.py:264
  32.1 3.3 %collective-permute-done.9.refs_2_ = bf16[128,256]{1,0:T(8,128)(2,1)S(1)} collective-permute-done((bf16[128,256]{1,0:T(8,128)(2,1)S(1)}, bf16[128,256]{1,0:T(8,128)(2,1)S(1)}, u32[]{:S(2)}, u32[]{:S(2)}) %collective-permute-start.9) | collective-permute-done | bytes 65568 | tf_op jit(solution)/shard_map/ppermute | solution.py:264
  35.5 0.1 collective-permute-done.10.refs_3_
  35.7 0.6 %collective-permute-start.11 = (bf16[1,64,256]{2,1,0:T(8,128)(2,1)S(1)}, bf16[1,64,256]{2,1,0:T(8,128)(2,1)S(1)}, u32[]{:S(2)}, u32[]{:S(2)}) collective-permute-start(bf16[1,64,256]{2,1,0:T(8,128)(2,1)S(1)} %get-tuple-element.64), channel_id=1, source_target_pairs={{0,1},{1,0},{2,3},{3,2},{4,5},{5,4},{6,7},{7,6},{8,9},{9,8},{10,11... | collective-permute-start | bytes 98312 | tf_op jit(solution)/shard_map/ppermute | solution.py:264
  36.3 0.0 collective-permute-done.13.value_in
  36.3 2.4 %collective-permute-start.14 = (bf16[64,256]{1,0:T(8,128)(2,1)S(1)}, bf16[64,256]{1,0:T(8,128)(2,1)S(1)}, u32[]{:S(2)}, u32[]{:S(2)}) collective-permute-start(bf16[64,256]{1,0:T(8,128)(2,1)S(1)} %get-tuple-element.70), channel_id=1, source_target_pairs={{0,4},{1,5},{2,6},{3,7},{4,0},{5,1},{6,2},{7,3},{8,12},{9,13},{10,... | collective-permute-start | bytes 98312 | tf_op jit(solution)/shard_map/ppermute | solution.py:264
  38.7 0.7 %collective-permute-start.15 = (bf16[64,256]{1,0:T(8,128)(2,1)S(1)}, bf16[64,256]{1,0:T(8,128)(2,1)S(1)}, u32[]{:S(2)}, u32[]{:S(2)}) collective-permute-start(bf16[64,256]{1,0:T(8,128)(2,1)S(1)} %get-tuple-element.71), channel_id=1, source_target_pairs={{0,6},{1,7},{2,4},{3,5},{4,2},{5,3},{6,0},{7,1},{8,14},{9,15},{10,... | collective-permute-start | bytes 98312 | tf_op jit(solution)/shard_map/ppermute | solution.py:264
  39.3 0.5 %collective-permute-start.16 = (bf16[64,256]{1,0:T(8,128)(2,1)S(1)}, bf16[64,256]{1,0:T(8,128)(2,1)S(1)}, u32[]{:S(2)}, u32[]{:S(2)}) collective-permute-start(bf16[64,256]{1,0:T(8,128)(2,1)S(1)} %get-tuple-element.72), channel_id=1, source_target_pairs={{0,2},{1,3},{2,0},{3,1},{4,6},{5,7},{6,4},{7,5},{8,10},{9,11},{10,... | collective-permute-start | bytes 98312 | tf_op jit(solution)/shard_map/ppermute | solution.py:264
  39.8 0.0 collective-permute-done.6
  39.8 0.8 %fusion = bf16[1,512,256]{2,1,0:T(8,128)(2,1)} fusion(f32[512,256]{1,0:T(8,128)S(1)} %get-tuple-element.55, bf16[512,256]{1,0:T(8,128)(2,1)S(1)} %collective-permute-done.6), kind=kLoop, calls=%fused_computation.1 | loop fusion | flops 524288 | bytes 1048576 | tf_op jit(solution)/shard_map/broadcast_in_dim | solution.py:370
  40.6 0.0 collective-permute-done.11.key_in
  40.6 0.9 %collective-permute-done.14.refs_1_ = bf16[64,256]{1,0:T(8,128)(2,1)S(1)} collective-permute-done((bf16[64,256]{1,0:T(8,128)(2,1)S(1)}, bf16[64,256]{1,0:T(8,128)(2,1)S(1)}, u32[]{:S(2)}, u32[]{:S(2)}) %collective-permute-start.14) | collective-permute-done | bytes 32800 | tf_op jit(solution)/shard_map/ppermute | solution.py:264
  41.5 2.9 %collective-permute-done.15.refs_2_ = bf16[64,256]{1,0:T(8,128)(2,1)S(1)} collective-permute-done((bf16[64,256]{1,0:T(8,128)(2,1)S(1)}, bf16[64,256]{1,0:T(8,128)(2,1)S(1)}, u32[]{:S(2)}, u32[]{:S(2)}) %collective-permute-start.15) | collective-permute-done | bytes 32800 | tf_op jit(solution)/shard_map/ppermute | solution.py:264
  44.4 0.0 collective-permute-done.16.refs_3_
  44.4 0.7 %shard_map.93 = (f32[1,64,256]{2,1,0:T(8,128)}, f32[1,64,256]{2,1,0:T(8,128)}) custom-call(f32[1,64,256]{2,1,0:T(8,128)S(1)} %get-tuple-element.63.key_mine, bf16[1,64,256]{2,1,0:T(8,128)(2,1)S(1)} %collective-permute-done.11.key_in, f32[64,256]{1,0:T(8,128)S(1)} %get-tuple-element.69.refs_0_, bf16[64,256]{1,0:T(8,128)(2,1)S(1)} %collective-permute-done.14.refs_1_, ...), custom_call_target="tpu_custom_call" | custom-call | flops 524288 | bytes 2048 | tf_op jit(solution)/shard_map/pallas_call | solution.py:272
  (2 shorter events, 0.1 us)
Async XLA Ops:
  0.6 9.4 %collective-permute-start = (bf16[512,256]{1,0:T(8,128)(2,1)}, bf16[512,256]{1,0:T(8,128)(2,1)S(1)}, u32[]{:S(2)}, u32[]{:S(2)}) collective-permute-start(bf16[512,256]{1,0:T(8,128)(2,1)} %bitcast.6), channel_id=1, source_target_pairs={{0,8},{8,0},{16,24},{24,16},{1,9},{9,1},{17,25},{25,17},{2,10},{10... | collective-permute-start | bytes 786440 | tf_op jit(solution)/shard_map/ppermute | solution.py:268
  1.2 8.8 %collective-permute-start.1 = (bf16[512,256]{1,0:T(8,128)(2,1)}, bf16[512,256]{1,0:T(8,128)(2,1)S(1)}, u32[]{:S(2)}, u32[]{:S(2)}) collective-permute-start(bf16[512,256]{1,0:T(8,128)(2,1)} %bitcast.8), channel_id=1, source_target_pairs={{0,8},{8,0},{16,24},{24,16},{1,9},{9,1},{17,25},{25,17},{2,10},{10... | collective-permute-start | bytes 786440 | tf_op jit(solution)/shard_map/ppermute | solution.py:268
  1.3 12.1 %collective-permute-start.2 = (bf16[512,256]{1,0:T(8,128)(2,1)}, bf16[512,256]{1,0:T(8,128)(2,1)S(1)}, u32[]{:S(2)}, u32[]{:S(2)}) collective-permute-start(bf16[512,256]{1,0:T(8,128)(2,1)} %bitcast.10), channel_id=1, source_target_pairs={{0,16},{8,24},{16,0},{24,8},{1,17},{9,25},{17,1},{25,9},{2,18},{10... | collective-permute-start | bytes 786440 | tf_op jit(solution)/shard_map/ppermute | solution.py:259
  4.2 12.5 %collective-permute-start.3 = (bf16[512,256]{1,0:T(8,128)(2,1)}, bf16[512,256]{1,0:T(8,128)(2,1)S(1)}, u32[]{:S(2)}, u32[]{:S(2)}) collective-permute-start(bf16[512,256]{1,0:T(8,128)(2,1)} %bitcast.12), channel_id=1, source_target_pairs={{0,16},{8,24},{16,0},{24,8},{1,17},{9,25},{17,1},{25,9},{2,18},{10... | collective-permute-start | bytes 786440 | tf_op jit(solution)/shard_map/ppermute | solution.py:259
  4.2 0.9 %copy-start = (bf16[1,512,256]{2,1,0:T(8,128)(2,1)S(1)}, bf16[1,512,256]{2,1,0:T(8,128)(2,1)}, u32[]{:S(2)}) copy-start(bf16[1,512,256]{2,1,0:T(8,128)(2,1)} %param.7) | copy-start | bytes 786436
  5.2 0.9 %copy-start.1 = (bf16[1,512,256]{2,1,0:T(8,128)(2,1)S(1)}, bf16[1,512,256]{2,1,0:T(8,128)(2,1)}, u32[]{:S(2)}) copy-start(bf16[1,512,256]{2,1,0:T(8,128)(2,1)} %param.8) | copy-start | bytes 786436
  6.1 0.9 %copy-start.2 = (bf16[1,512,256]{2,1,0:T(8,128)(2,1)S(1)}, bf16[1,512,256]{2,1,0:T(8,128)(2,1)}, u32[]{:S(2)}) copy-start(bf16[1,512,256]{2,1,0:T(8,128)(2,1)} %param.6) | copy-start | bytes 786436
  7.1 0.9 %copy-start.3 = (bf16[1,512,256]{2,1,0:T(8,128)(2,1)S(1)}, bf16[1,512,256]{2,1,0:T(8,128)(2,1)}, u32[]{:S(2)}) copy-start(bf16[1,512,256]{2,1,0:T(8,128)(2,1)} %param.9) | copy-start | bytes 786436
  8.0 0.7 %copy-start.4 = (s32[1,8]{1,0:T(1,128)S(1)}, s32[1,8]{1,0:T(1,128)}, u32[]{:S(2)}) copy-start(s32[1,8]{1,0:T(1,128)} %docs.1) | copy-start | bytes 100
  8.7 0.7 %copy-start.5 = (s32[8]{0:T(128)S(1)}, s32[8]{0:T(128)}, u32[]{:S(2)}) copy-start(s32[8]{0:T(128)} %fold.1) | copy-start | bytes 100
  11.6 7.8 %collective-permute-start.5 = (f32[3,512]{1,0:T(4,128)S(1)}, f32[3,512]{1,0:T(4,128)S(1)}, u32[]{:S(2)}, u32[]{:S(2)}) collective-permute-start(f32[3,512]{1,0:T(4,128)S(1)} %get-tuple-element.47.refs_2_), channel_id=1, source_target_pairs={{0,16},{8,24},{16,0},{24,8},{1,17},{9,25},{17,1},{25,9},{2,18},{10... | collective-permute-start | bytes 18440 | tf_op jit(solution)/shard_map/ppermute | solution.py:259
  17.3 3.8 %collective-permute-start.4 = (f32[3,512]{1,0:T(4,128)S(1)}, f32[3,512]{1,0:T(4,128)S(1)}, u32[]{:S(2)}, u32[]{:S(2)}) collective-permute-start(f32[3,512]{1,0:T(4,128)S(1)} %get-tuple-element.50.refs_2_), channel_id=1, source_target_pairs={{0,16},{8,24},{16,0},{24,8},{1,17},{9,25},{17,1},{25,9},{2,18},{10... | collective-permute-start | bytes 18440 | tf_op jit(solution)/shard_map/ppermute | solution.py:259
  22.6 2.4 %collective-permute-start.12 = (bf16[512,256]{1,0:T(8,128)(2,1)S(1)}, bf16[512,256]{1,0:T(8,128)(2,1)S(1)}, u32[]{:S(2)}, u32[]{:S(2)}) collective-permute-start(bf16[512,256]{1,0:T(8,128)(2,1)S(1)} %get-tuple-element.66), channel_id=1, source_target_pairs={{0,8},{8,0},{16,24},{24,16},{1,9},{9,1},{17,25},{25,17},{2,10},{10... | collective-permute-start | bytes 786440 | tf_op jit(solution)/shard_map/ppermute | solution.py:268
  22.7 3.9 %collective-permute-start.7 = (bf16[512,256]{1,0:T(8,128)(2,1)S(1)}, bf16[512,256]{1,0:T(8,128)(2,1)S(1)}, u32[]{:S(2)}, u32[]{:S(2)}) collective-permute-start(bf16[512,256]{1,0:T(8,128)(2,1)S(1)} %get-tuple-element.58), channel_id=1, source_target_pairs={{0,8},{8,0},{16,24},{24,16},{1,9},{9,1},{17,25},{25,17},{2,10},{10... | collective-permute-start | bytes 786440 | tf_op jit(solution)/shard_map/ppermute | solution.py:268
  23.2 16.7 %collective-permute-start.6 = (bf16[512,256]{1,0:T(8,128)(2,1)S(1)}, bf16[512,256]{1,0:T(8,128)(2,1)S(1)}, u32[]{:S(2)}, u32[]{:S(2)}) collective-permute-start(bf16[512,256]{1,0:T(8,128)(2,1)S(1)} %get-tuple-element.56), channel_id=1, source_target_pairs={{0,16},{8,24},{16,0},{24,8},{1,17},{9,25},{17,1},{25,9},{2,18},{10... | collective-permute-start | bytes 786440 | tf_op jit(solution)/shard_map/ppermute | solution.py:259
  25.0 11.3 %collective-permute-start.13 = (bf16[4,64,256]{2,1,0:T(8,128)(2,1)S(1)}, bf16[4,64,256]{2,1,0:T(8,128)(2,1)S(1)}, u32[]{:S(2)}, u32[]{:S(2)}) collective-permute-start(bf16[4,64,256]{2,1,0:T(8,128)(2,1)S(1)} %get-tuple-element.68), channel_id=1, source_target_pairs={{0,1},{1,0},{2,3},{3,2},{4,5},{5,4},{6,7},{7,6},{8,9},{9,8},{10,11... | collective-permute-start | bytes 393224 | tf_op jit(solution)/shard_map/ppermute | solution.py:264
  26.6 5.5 %collective-permute-start.8 = (bf16[128,256]{1,0:T(8,128)(2,1)S(1)}, bf16[128,256]{1,0:T(8,128)(2,1)S(1)}, u32[]{:S(2)}, u32[]{:S(2)}) collective-permute-start(bf16[128,256]{1,0:T(8,128)(2,1)S(1)} %get-tuple-element.60), channel_id=1, source_target_pairs={{0,4},{1,5},{2,6},{3,7},{4,0},{5,1},{6,2},{7,3},{8,12},{9,13},{10,... | collective-permute-start | bytes 196616 | tf_op jit(solution)/shard_map/ppermute | solution.py:264
  29.3 6.2 %collective-permute-start.9 = (bf16[128,256]{1,0:T(8,128)(2,1)S(1)}, bf16[128,256]{1,0:T(8,128)(2,1)S(1)}, u32[]{:S(2)}, u32[]{:S(2)}) collective-permute-start(bf16[128,256]{1,0:T(8,128)(2,1)S(1)} %get-tuple-element.61), channel_id=1, source_target_pairs={{0,6},{1,7},{2,4},{3,5},{4,2},{5,3},{6,0},{7,1},{8,14},{9,15},{10,... | collective-permute-start | bytes 196616 | tf_op jit(solution)/shard_map/ppermute | solution.py:264
  30.6 5.0 %collective-permute-start.10 = (bf16[128,256]{1,0:T(8,128)(2,1)S(1)}, bf16[128,256]{1,0:T(8,128)(2,1)S(1)}, u32[]{:S(2)}, u32[]{:S(2)}) collective-permute-start(bf16[128,256]{1,0:T(8,128)(2,1)S(1)} %get-tuple-element.62), channel_id=1, source_target_pairs={{0,2},{1,3},{2,0},{3,1},{4,6},{5,7},{6,4},{7,5},{8,10},{9,11},{10,... | collective-permute-start | bytes 196616 | tf_op jit(solution)/shard_map/ppermute | solution.py:264
  35.7 5.0 %collective-permute-start.11 = (bf16[1,64,256]{2,1,0:T(8,128)(2,1)S(1)}, bf16[1,64,256]{2,1,0:T(8,128)(2,1)S(1)}, u32[]{:S(2)}, u32[]{:S(2)}) collective-permute-start(bf16[1,64,256]{2,1,0:T(8,128)(2,1)S(1)} %get-tuple-element.64), channel_id=1, source_target_pairs={{0,1},{1,0},{2,3},{3,2},{4,5},{5,4},{6,7},{7,6},{8,9},{9,8},{10,11... | collective-permute-start | bytes 98312 | tf_op jit(solution)/shard_map/ppermute | solution.py:264
  36.3 5.2 %collective-permute-start.14 = (bf16[64,256]{1,0:T(8,128)(2,1)S(1)}, bf16[64,256]{1,0:T(8,128)(2,1)S(1)}, u32[]{:S(2)}, u32[]{:S(2)}) collective-permute-start(bf16[64,256]{1,0:T(8,128)(2,1)S(1)} %get-tuple-element.70), channel_id=1, source_target_pairs={{0,4},{1,5},{2,6},{3,7},{4,0},{5,1},{6,2},{7,3},{8,12},{9,13},{10,... | collective-permute-start | bytes 98312 | tf_op jit(solution)/shard_map/ppermute | solution.py:264
  38.7 5.7 %collective-permute-start.15 = (bf16[64,256]{1,0:T(8,128)(2,1)S(1)}, bf16[64,256]{1,0:T(8,128)(2,1)S(1)}, u32[]{:S(2)}, u32[]{:S(2)}) collective-permute-start(bf16[64,256]{1,0:T(8,128)(2,1)S(1)} %get-tuple-element.71), channel_id=1, source_target_pairs={{0,6},{1,7},{2,4},{3,5},{4,2},{5,3},{6,0},{7,1},{8,14},{9,15},{10,... | collective-permute-start | bytes 98312 | tf_op jit(solution)/shard_map/ppermute | solution.py:264
  39.3 5.1 %collective-permute-start.16 = (bf16[64,256]{1,0:T(8,128)(2,1)S(1)}, bf16[64,256]{1,0:T(8,128)(2,1)S(1)}, u32[]{:S(2)}, u32[]{:S(2)}) collective-permute-start(bf16[64,256]{1,0:T(8,128)(2,1)S(1)} %get-tuple-element.72), channel_id=1, source_target_pairs={{0,2},{1,3},{2,0},{3,1},{4,6},{5,7},{6,4},{7,5},{8,10},{9,11},{10,... | collective-permute-start | bytes 98312 | tf_op jit(solution)/shard_map/ppermute | solution.py:264
